TPU v7x, 16 devices: a whole 2x2x2 slice. The times are simulated.
16 devices in a mesh: col: 2 (over z), row: 8 (over y, x, core).
Axes of the slice: x: 2, y: 2, z: 2, core: 2. Of those that a mesh axis runs over, the one named last changes fastest.
Arguments:
- vel_u: float32 [31, 256, 1024], P(None, 'row', 'col')
- vel_v: float32 [31, 256, 1024], P(None, 'row', 'col')
- temperature: float32 [31, 256, 1024], P(None, 'row', 'col')
- salinity: float32 [31, 256, 1024], P(None, 'row', 'col')
- surf_eta: float32 [256, 1024], P('row', 'col')
- trans_u: float32 [256, 1024], P('row', 'col')
- trans_v: float32 [256, 1024], P('row', 'col')
- bottom_depth: float32 [256, 1024], P('row', 'col')
- level_count: int32 [256, 1024], P('row', 'col')
- avg_weights: float32 [30], replicated
Outputs:
- output 1: float32 [256, 1024], P('row', 'col')
- output 2: float32 [256, 1024], P('row', 'col')
- output 3: float32 [256, 1024], P('row', 'col')
- output 4: float32 [31, 256, 1024], P(None, 'row', 'col')
- output 5: float32 [31, 256, 1024], P(None, 'row', 'col')
- output 6: float32 [31, 256, 1024], P(None, 'row', 'col')
- output 7: float32 [31, 256, 1024], P(None, 'row', 'col')
All inputs are finite; a program needn't handle non-finite values.
Results may differ from a plain program's by a relative error of at most 0.001.
Values sent between devices are 32-bit elements.
A program may use at most 1 GiB of HBM per device.

v0:
```python
import jax
import jax.numpy as jnp
from jax import lax
from jax.sharding import PartitionSpec as P

TIME_STEP = 1.0
GRAVITY = 16.0
BC_GRAVITY = 4.0
EXPAND_T = 0.2
CONTRACT_S = 0.6
CORIO_F0 = 0.4
CORIO_BETA = 0.4
VISC_R = 2.0
DIFF_R = 0.5


def shifted(padded, step_y, step_x):
    n_rows = padded.shape[-2] - 2
    n_cols = padded.shape[-1] - 2
    return padded[..., 1 + step_y:1 + step_y + n_rows, 1 + step_x:1 + step_x + n_cols]


def tri_solve(right_side, active, strength):
    link = strength * active[1:]
    zero_row = jnp.zeros_like(right_side[:1])
    low_links = jnp.concatenate([zero_row, link], axis=0)
    up_links = jnp.concatenate([link, zero_row], axis=0)

    def down(carry, level):
        ratio_prev, value_prev = carry
        low_link, up_link, target = level
        denominator = 1.0 + low_link + up_link + low_link * ratio_prev
        ratio = -up_link / denominator
        value = (target + low_link * value_prev) / denominator
        return (ratio, value), (ratio, value)

    start = (jnp.zeros_like(right_side[0]), jnp.zeros_like(right_side[0]))
    _, (ratios, values) = lax.scan(down, start, (low_links, up_links, right_side))

    def back(below, level):
        ratio, value = level
        solved = value - ratio * below
        return solved, solved

    _, solved_all = lax.scan(back, jnp.zeros_like(right_side[0]), (ratios, values), reverse=True)
    return solved_all


def ocean_columns(u_pad, v_pad, array_b15, salinity_pad, count_pad, depth_pad, coriolis_u, coriolis_v):
    n_levels = u_pad.shape[0]
    count_mid = shifted(count_pad, 0, 0)
    levels_u = jnp.minimum(count_mid, shifted(count_pad, 0, 1))
    levels_uw = jnp.minimum(shifted(count_pad, 0, -1), count_mid)
    levels_v = jnp.minimum(count_mid, shifted(count_pad, 1, 0))
    levels_vs = jnp.minimum(shifted(count_pad, -1, 0), count_mid)
    level_index = jnp.arange(n_levels)[:, None, None]
    mask_mid = (level_index < count_mid).astype(jnp.float32)
    mask_u = (level_index < levels_u).astype(jnp.float32)
    mask_uw = (level_index < levels_uw).astype(jnp.float32)
    mask_v = (level_index < levels_v).astype(jnp.float32)
    mask_vs = (level_index < levels_vs).astype(jnp.float32)
    u_mid = shifted(u_pad, 0, 0)
    v_mid = shifted(v_pad, 0, 0)
    u_west = shifted(u_pad, 0, -1)
    v_south = shifted(v_pad, -1, 0)
    v_at_u = 0.25 * (v_mid + shifted(v_pad, 0, 1) + v_south + shifted(v_pad, -1, 1))
    u_at_v = 0.25 * (u_mid + u_west + shifted(u_pad, 1, 0) + shifted(u_pad, 1, -1))
    inertia_u = 0.5 * (u_mid * (shifted(u_pad, 0, 1) - u_west) + v_at_u * (shifted(u_pad, 1, 0) - shifted(u_pad, -1, 0)))
    inertia_v = 0.5 * (u_at_v * (shifted(v_pad, 0, 1) - shifted(v_pad, 0, -1)) + v_mid * (shifted(v_pad, 1, 0) - v_south))
    density = CONTRACT_S * salinity_pad - EXPAND_T * array_b15
    pressure = (BC_GRAVITY / n_levels) * (jnp.cumsum(density, axis=0) - 0.5 * density)
    pressure_mid = shifted(pressure, 0, 0)
    u_star = u_mid + TIME_STEP * (coriolis_u * v_at_u - inertia_u - shifted(pressure, 0, 1) + pressure_mid)
    v_star = v_mid + TIME_STEP * (-coriolis_v * u_at_v - inertia_v - shifted(pressure, 1, 0) + pressure_mid)
    u_visc = tri_solve(u_star, mask_u, VISC_R)
    v_visc = tri_solve(v_star, mask_v, VISC_R)
    count_u = jnp.maximum(jnp.sum(mask_u, axis=0), 1.0)
    count_v = jnp.maximum(jnp.sum(mask_v, axis=0), 1.0)
    depth_mid = shifted(depth_pad, 0, 0)
    depth_u = 0.5 * (depth_mid + shifted(depth_pad, 0, 1))
    depth_v = 0.5 * (depth_mid + shifted(depth_pad, 1, 0))
    force_u = depth_u * jnp.sum(mask_u * (u_visc - u_mid), axis=0) / count_u / TIME_STEP
    force_v = depth_v * jnp.sum(mask_v * (v_visc - v_mid), axis=0) / count_v / TIME_STEP
    shear_u = u_visc - jnp.sum(mask_u * u_visc, axis=0) / count_u
    shear_v = v_visc - jnp.sum(mask_v * v_visc, axis=0) / count_v
    wet_u = (levels_u > 0).astype(jnp.float32)
    wet_v = (levels_v > 0).astype(jnp.float32)

    def advect(tracer_pad):
        tracer_mid = shifted(tracer_pad, 0, 0)
        flux_east = mask_u * u_mid * (tracer_mid + shifted(tracer_pad, 0, 1))
        flux_west = mask_uw * u_west * (shifted(tracer_pad, 0, -1) + tracer_mid)
        flux_north = mask_v * v_mid * (tracer_mid + shifted(tracer_pad, 1, 0))
        flux_south = mask_vs * v_south * (shifted(tracer_pad, -1, 0) + tracer_mid)
        return tracer_mid - 0.5 * TIME_STEP * (flux_east - flux_west + flux_north - flux_south)

    value_a15 = tri_solve(advect(array_b15), mask_mid, DIFF_R)
    salinity_new = tri_solve(advect(salinity_pad), mask_mid, DIFF_R)
    return (shear_u, shear_v, mask_u, mask_v, depth_u, depth_v, wet_u, wet_v, force_u, force_v, value_a15, salinity_new)


def fast_update(stack_pad, force_u, force_v, depth_u, depth_v, wet_u, wet_v, coriolis_u, coriolis_v, dt_fast):
    eta_pad = stack_pad[0]
    trans_u_pad = stack_pad[1]
    trans_v_pad = stack_pad[2]
    eta_ext = eta_pad[1:, 1:] - dt_fast * (trans_u_pad[1:, 1:] - trans_u_pad[1:, :-1] + trans_v_pad[1:, 1:] - trans_v_pad[:-1, 1:])
    eta_new = eta_ext[:-1, :-1]
    trans_u_old = shifted(trans_u_pad, 0, 0)
    trans_v_old = shifted(trans_v_pad, 0, 0)
    v_at_u = 0.25 * (trans_v_old + shifted(trans_v_pad, 0, 1) + shifted(trans_v_pad, -1, 0) + shifted(trans_v_pad, -1, 1))
    u_at_v = 0.25 * (trans_u_old + shifted(trans_u_pad, 0, -1) + shifted(trans_u_pad, 1, 0) + shifted(trans_u_pad, 1, -1))
    trans_u_new = wet_u * (trans_u_old + dt_fast * (coriolis_u * v_at_u + force_u - GRAVITY * depth_u * (eta_ext[:-1, 1:] - eta_new)))
    trans_v_new = wet_v * (trans_v_old + dt_fast * (force_v - coriolis_v * u_at_v - GRAVITY * depth_v * (eta_ext[1:, :-1] - eta_new)))
    return eta_new, trans_u_new, trans_v_new


def solution(mesh):
    n_col = mesh.shape['col']
    n_row = mesh.shape['row']
    east_moves = [(index, (index + 1) % n_col) for index in range(n_col)]
    west_moves = [(index, (index - 1) % n_col) for index in range(n_col)]
    north_moves = [(index, index + 1) for index in range(n_row - 1)]
    south_moves = [(index + 1, index) for index in range(n_row - 1)]

    def exchange(field):
        from_west = lax.ppermute(field[..., -1:], 'col', east_moves)
        from_east = lax.ppermute(field[..., :1], 'col', west_moves)
        wide = jnp.concatenate([from_west, field, from_east], axis=-1)
        from_south = lax.ppermute(wide[..., -1:, :], 'row', north_moves)
        from_north = lax.ppermute(wide[..., :1, :], 'row', south_moves)
        return jnp.concatenate([from_south, wide, from_north], axis=-2)

    def step(vel_u, vel_v, value_a11, salinity, surf_eta, trans_u, trans_v, bottom_depth, level_count, avg_weights):
        n_rows = surf_eta.shape[0]
        total_rows = n_rows * n_row
        dt_fast = TIME_STEP / avg_weights.shape[0]
        row_pos = (lax.axis_index('row') * n_rows + jnp.arange(n_rows)).astype(jnp.float32)[:, None]
        coriolis_u = CORIO_F0 + CORIO_BETA * ((row_pos + 0.5) / total_rows - 0.5)
        coriolis_v = CORIO_F0 + CORIO_BETA * ((row_pos + 1.0) / total_rows - 0.5)
        columns = ocean_columns(exchange(vel_u), exchange(vel_v), exchange(value_a11), exchange(salinity), exchange(level_count), exchange(bottom_depth), coriolis_u, coriolis_v)
        shear_u, shear_v, mask_u, mask_v, depth_u, depth_v, wet_u, wet_v, force_u, force_v, value_a15, salinity_new = columns

        def subcycle(carry, weight):
            eta_old, trans_u_old, trans_v_old, acc_u, acc_v = carry
            stack_pad = exchange(jnp.stack([eta_old, trans_u_old, trans_v_old]))
            eta_new, trans_u_new, trans_v_new = fast_update(stack_pad, force_u, force_v, depth_u, depth_v, wet_u, wet_v, coriolis_u, coriolis_v, dt_fast)
            return (eta_new, trans_u_new, trans_v_new, acc_u + weight * trans_u_new, acc_v + weight * trans_v_new), None

        zero_field = jnp.zeros_like(surf_eta)
        final, _ = lax.scan(subcycle, (surf_eta, trans_u, trans_v, zero_field, zero_field), avg_weights)
        eta_fin, trans_u_fin, trans_v_fin, bar_u, bar_v = final
        vel_u_new = mask_u * (shear_u + bar_u / depth_u)
        vel_v_new = mask_v * (shear_v + bar_v / depth_v)
        return (eta_fin, trans_u_fin, trans_v_fin, vel_u_new, vel_v_new, value_a15, salinity_new)

    cube = P(None, 'row', 'col')
    flat = P('row', 'col')
    return jax.shard_map(step, mesh=mesh, in_specs=(cube, cube, cube, cube, flat, flat, flat, flat, flat, P()), out_specs=(flat, flat, flat, cube, cube, cube, cube), check_vma=False)
```

profile of v0, /device:TPU:4, one launch (start us, length us, event | category | flops | bytes accessed | tf_op | source)
XLA Modules:
  0.0 1057.7 jit_solution(345823658337436664)
XLA Ops:
  19.6 21.3 %collective-permute-done.21 = f32[32,1]{1,0:T(8,128)S(1)} collective-permute-done((f32[32,1]{1,0:T(8,128)S(1)}, f32[32,1]{1,0:T(8,128)S(1)}, u32[]{:S(2)}, u32[]{:S(2)}) %collective-permute-start.21) | collective-permute-done | bytes 160 | tf_op jit(solution)/shard_map/ppermute | solution.py:126
  60.7 3.8 collective-permute-done.14
  64.9 3.3 collective-permute-start.22
  68.2 18.0 %collective-permute-done.17 = f32[31,32,1]{2,1,0:T(8,128)S(1)} collective-permute-done((f32[31,32,1]{2,1,0:T(8,128)S(1)}, f32[31,32,1]{2,1,0:T(8,128)S(1)}, u32[]{:S(2)}, u32[]{:S(2)}) %collective-permute-start.17) | collective-permute-done | bytes 4000 | tf_op jit(solution)/shard_map/ppermute | solution.py:126
  88.5 8.6 collective-permute-done.18
  100.5 4.2 collective-permute-start.16
  104.7 3.3 collective-permute-done.9
  113.5 4.4 collective-permute-start.20
  120.0 5.7 fusion.47
  128.8 52.6 %while.163 = (s32[]{:T(128)}, f32[32,512]{1,0:T(8,128)}, f32[32,512]{1,0:T(8,128)}, f32[31,32,512]{2,1,0:T(8,128)}, f32[31,32,512]{2,1,0:T(8,128)}, /*index=5*/f...) while((s32[]{:T(128)}, f32[32,512]{1,0:T(8,128)}, ...), condition=%wide.region_22.23_spmd.clone, body=%wide.region_21.22_spmd.clone.sunk | while | flops 180227 | bytes 590447 | solution.py:38
  182.9 48.6 %while.164 = (s32[]{:T(128)}, f32[32,512]{1,0:T(8,128)}, f32[31,32,512]{2,1,0:T(8,128)}, f32[31,32,512]{2,1,0:T(8,128)}, f32[31,32,512]{2,1,0:T(8,128)}, /*index=5*/s32[]{:T(128)}, s32[]{:T(128)}, s32[]{:T(128)}) while((s32[]{:T(128)}, f32[32,512]{1,0:T(8,128)}, f32[31,32,512]{2,1,0:T(8,128)}, f32[31,32,512]{2,1,0:T(8,128)}, ...), condition=%wide.region_24.25_spmd.clone, body=%wide.region_23.24_spmd.clone.sunk | while | flops 49156 | bytes 327791 | solution.py:45
  233.9 4.1 collective-permute-start.25
  238.0 12.0 %fusion.60 = f32[31,32,512]{2,1,0:T(8,128)} fusion(f32[31,32,512]{2,1,0:T(8,128)} %param.30, f32[31,1,514]{2,1,0:T(1,128)} %collective-permute-done.19, f32[31,32,1]{2,1,0:T(8,128)} %copy-done.18, f32[31,32,1]{2,1,0:T(8,128)} %copy-done.17, f32[31,1,514]{2,1,0:T(1,128)} %collective-permute-done.20, f32[31,32,512]{2,1,0:T(8,128)S(1)} %copy-done, ...), kind=kLoop, calls=%fused_computation.136 | loop fusion | flops 15237120 | bytes 10559600 | tf_op jit(solution)/shard_map/sub | solution.py:95
  253.2 52.6 %while.161 = (s32[]{:T(128)}, f32[32,512]{1,0:T(8,128)}, f32[32,512]{1,0:T(8,128)}, f32[31,32,512]{2,1,0:T(8,128)}, f32[31,32,512]{2,1,0:T(8,128)}, /*index=5*/f...) while((s32[]{:T(128)}, f32[32,512]{1,0:T(8,128)}, ...), condition=%wide.region_18.19_spmd.clone, body=%wide.region_17.18_spmd.clone.sunk | while | flops 180227 | bytes 590447 | solution.py:38
  307.3 48.6 %while.162 = (s32[]{:T(128)}, f32[32,512]{1,0:T(8,128)}, f32[31,32,512]{2,1,0:T(8,128)}, f32[31,32,512]{2,1,0:T(8,128)}, f32[31,32,512]{2,1,0:T(8,128)}, /*index=5*/s32[]{:T(128)}, s32[]{:T(128)}, s32[]{:T(128)}) while((s32[]{:T(128)}, f32[32,512]{1,0:T(8,128)}, f32[31,32,512]{2,1,0:T(8,128)}, f32[31,32,512]{2,1,0:T(8,128)}, ...), condition=%wide.region_20.21_spmd.clone, body=%wide.region_19.20_spmd.clone.sunk | while | flops 49156 | bytes 327791 | solution.py:45
  355.9 10.9 %subtract_multiply_fusion = f32[31,34,514]{2,1,0:T(8,128)} fusion(f32[31,1,514]{2,1,0:T(1,128)} %collective-permute-done.20, f32[31,32,1]{2,1,0:T(8,128)} %copy-done.18, f32[31,32,512]{2,1,0:T(8,128)} %param.30, f32[31,32,1]{2,1,0:T(8,128)} %copy-done.17, f32[31,1,514]{2,1,0:T(1,128)} %collective-permute-done.19, f32[31,1,514]{2,1,0:T(1,128)} %copy-done.38, ...), kind=kOutput, calls=%fused_computation.109 | output fusion | flops 29796580 | bytes 6501072 | tf_op jit(solution)/shard_map/jit(cumsum)/reduce_window_sum | solution.py:71
  369.6 9.9 fusion.79
  382.6 49.6 %while.157 = (s32[]{:T(128)}, f32[32,512]{1,0:T(8,128)S(1)}, f32[32,512]{1,0:T(8,128)S(1)}, f32[31,32,512]{2,1,0:T(8,128)}, f32[31,32,512]{2,1,0:T(8,128)}, /*in...) while((s32[]{:T(128)}, f32[32,512]{1,0:T(8,128)S(1)}, ...), condition=%wide.region_2.3_spmd.clone, body=%wide.region_1.2_spmd.clone.sunk | while | flops 180227 | bytes 590447 | solution.py:38
  433.8 47.6 %while.158 = (s32[]{:T(128)}, f32[32,512]{1,0:T(8,128)S(1)}, f32[31,32,512]{2,1,0:T(8,128)}, f32[31,32,512]{2,1,0:T(8,128)}, f32[31,32,512]{2,1,0:T(8,128)}, /*index=5*/s32[]{:T(128)}, s32[]{:T(128)}, s32[]{:T(128)}) while((s32[]{:T(128)}, f32[32,512]{1,0:T(8,128)S(1)}, f32[31,32,512]{2,1,0:T(8,128)}, f32[31,32,512]{2,1,0:T(8,128)}, ...), condition=%wide.region_4.5_spmd.clone, body=%wide.region_3.4_spmd.clone.sunk | while | flops 49156 | bytes 327791 | solution.py:45
  483.6 10.5 fusion.70
  497.2 49.6 %while.159 = (s32[]{:T(128)}, f32[32,512]{1,0:T(8,128)S(1)}, f32[32,512]{1,0:T(8,128)S(1)}, f32[31,32,512]{2,1,0:T(8,128)}, f32[31,32,512]{2,1,0:T(8,128)}, /*in...) while((s32[]{:T(128)}, f32[32,512]{1,0:T(8,128)S(1)}, ...), condition=%wide.region_8.9_spmd.clone, body=%wide.region_7.8_spmd.clone.sunk | while | flops 180227 | bytes 590447 | solution.py:38
  548.3 47.9 %while.160 = (s32[]{:T(128)}, f32[32,512]{1,0:T(8,128)S(1)}, f32[31,32,512]{2,1,0:T(8,128)}, f32[31,32,512]{2,1,0:T(8,128)}, f32[31,32,512]{2,1,0:T(8,128)}, /*index=5*/s32[]{:T(128)}, s32[]{:T(128)}, s32[]{:T(128)}) while((s32[]{:T(128)}, f32[32,512]{1,0:T(8,128)S(1)}, f32[31,32,512]{2,1,0:T(8,128)}, f32[31,32,512]{2,1,0:T(8,128)}, ...), condition=%wide.region_10.11_spmd.clone, body=%wide.region_9.10_spmd.clone.sunk | while | flops 49156 | bytes 327791 | solution.py:45
  599.5 453.5 %while.165 = (s32[]{:T(128)}, f32[32,512]{1,0:T(8,128)S(1)}, f32[32,512]{1,0:T(8,128)S(1)}, f32[32,512]{1,0:T(8,128)S(1)}, f32[32,512]{1,0:T(8,128)S(1)}, /*inde...) while((s32[]{:T(128)}, f32[32,512]{1,0:T(8,128)S(1)}, ...), condition=%wide.region_14.15_spmd.clone.clone.clone, body=%wide.region_13.14_spmd.clone.clone.clone.sunk | while | flops 903904 | bytes 3474976 | solution.py:150
  1053.2 4.3 add_select_fusion
  (952 shorter events, 929.6 us)
Async XLA Ops:
  1.5 16.0 %collective-permute-start.23 = (s32[32,1]{1,0:T(8,128)S(1)}, s32[32,1]{1,0:T(8,128)S(1)}, u32[]{:S(2)}, u32[]{:S(2)}) collective-permute-start(s32[32,1]{1,0:T(8,128)S(1)} %get-tuple-element.1216), channel_id=1, source_target_pairs={{0,8},{8,0},{1,9},{9,1},{2,10},{10,2},{3,11},{11,3},{4,12},{12,4},... | collective-permute-start | bytes 392 | tf_op jit(solution)/shard_map/ppermute | solution.py:126
  3.1 14.9 %collective-permute-start.5 = (s32[32,1]{1,0:T(8,128)S(1)}, s32[32,1]{1,0:T(8,128)S(1)}, u32[]{:S(2)}, u32[]{:S(2)}) collective-permute-start(s32[32,1]{1,0:T(8,128)S(1)} %get-tuple-element.1217), channel_id=1, source_target_pairs={{0,8},{8,0},{1,9},{9,1},{2,10},{10,2},{3,11},{11,3},{4,12},{12,4},... | collective-permute-start | bytes 392 | tf_op jit(solution)/shard_map/ppermute | solution.py:127
  5.8 49.0 %collective-permute-start.6 = (f32[31,32,1]{2,1,0:T(8,128)}, f32[31,32,1]{2,1,0:T(8,128)}, u32[]{:S(2)}, u32[]{:S(2)}) collective-permute-start(f32[31,32,1]{2,1,0:T(8,128)} %get-tuple-element.1191), channel_id=1, source_target_pairs={{0,8},{8,0},{1,9},{9,1},{2,10},{10,2},{3,11},{11,3},{4,12},{12,4},... | collective-permute-start | bytes 11912 | tf_op jit(solution)/shard_map/ppermute | solution.py:127
  7.4 49.0 %collective-permute-start.7 = (f32[31,32,1]{2,1,0:T(8,128)}, f32[31,32,1]{2,1,0:T(8,128)}, u32[]{:S(2)}, u32[]{:S(2)}) collective-permute-start(f32[31,32,1]{2,1,0:T(8,128)} %get-tuple-element.1190), channel_id=1, source_target_pairs={{0,8},{8,0},{1,9},{9,1},{2,10},{10,2},{3,11},{11,3},{4,12},{12,4},... | collective-permute-start | bytes 11912 | tf_op jit(solution)/shard_map/ppermute | solution.py:126
  15.9 43.2 %collective-permute-start.13 = (f32[31,32,1]{2,1,0:T(8,128)S(1)}, f32[31,32,1]{2,1,0:T(8,128)S(1)}, u32[]{:S(2)}, u32[]{:S(2)}) collective-permute-start(f32[31,32,1]{2,1,0:T(8,128)S(1)} %get-tuple-element.1196), channel_id=1, source_target_pairs={{0,8},{8,0},{1,9},{9,1},{2,10},{10,2},{3,11},{11,3},{4,12},{12,4},... | collective-permute-start | bytes 11912 | tf_op jit(solution)/shard_map/ppermute | solution.py:126
  17.5 23.4 %collective-permute-start.21 = (f32[32,1]{1,0:T(8,128)S(1)}, f32[32,1]{1,0:T(8,128)S(1)}, u32[]{:S(2)}, u32[]{:S(2)}) collective-permute-start(f32[32,1]{1,0:T(8,128)S(1)} %get-tuple-element.1214), channel_id=1, source_target_pairs={{0,8},{8,0},{1,9},{9,1},{2,10},{10,2},{3,11},{11,3},{4,12},{12,4},... | collective-permute-start | bytes 392 | tf_op jit(solution)/shard_map/ppermute | solution.py:126
  18.0 24.8 %collective-permute-start.4 = (f32[32,1]{1,0:T(8,128)S(1)}, f32[32,1]{1,0:T(8,128)S(1)}, u32[]{:S(2)}, u32[]{:S(2)}) collective-permute-start(f32[32,1]{1,0:T(8,128)S(1)} %get-tuple-element.1215), channel_id=1, source_target_pairs={{0,8},{8,0},{1,9},{9,1},{2,10},{10,2},{3,11},{11,3},{4,12},{12,4},... | collective-permute-start | bytes 392 | tf_op jit(solution)/shard_map/ppermute | solution.py:127
  43.5 8.2 collective-permute-start.26
  50.1 14.3 %collective-permute-start.14 = (f32[31,32,1]{2,1,0:T(8,128)S(1)}, f32[31,32,1]{2,1,0:T(8,128)S(1)}, u32[]{:S(2)}, u32[]{:S(2)}) collective-permute-start(f32[31,32,1]{2,1,0:T(8,128)S(1)} %get-tuple-element.1197), channel_id=1, source_target_pairs={{0,8},{8,0},{1,9},{9,1},{2,10},{10,2},{3,11},{11,3},{4,12},{12,4},... | collective-permute-start | bytes 11912 | tf_op jit(solution)/shard_map/ppermute | solution.py:127
  54.4 46.1 %collective-permute-start.10 = (f32[31,32,1]{2,1,0:T(8,128)S(1)}, f32[31,32,1]{2,1,0:T(8,128)S(1)}, u32[]{:S(2)}, u32[]{:S(2)}) collective-permute-start(f32[31,32,1]{2,1,0:T(8,128)S(1)} %get-tuple-element.1192), channel_id=1, source_target_pairs={{0,8},{8,0},{1,9},{9,1},{2,10},{10,2},{3,11},{11,3},{4,12},{12,4},... | collective-permute-start | bytes 11912 | tf_op jit(solution)/shard_map/ppermute | solution.py:126
  54.8 31.3 %collective-permute-start.17 = (f32[31,32,1]{2,1,0:T(8,128)S(1)}, f32[31,32,1]{2,1,0:T(8,128)S(1)}, u32[]{:S(2)}, u32[]{:S(2)}) collective-permute-start(f32[31,32,1]{2,1,0:T(8,128)S(1)} %get-tuple-element.1194), channel_id=1, source_target_pairs={{0,8},{8,0},{1,9},{9,1},{2,10},{10,2},{3,11},{11,3},{4,12},{12,4},... | collective-permute-start | bytes 11912 | tf_op jit(solution)/shard_map/ppermute | solution.py:126
  58.6 38.5 %collective-permute-start.18 = (f32[31,32,1]{2,1,0:T(8,128)S(1)}, f32[31,32,1]{2,1,0:T(8,128)S(1)}, u32[]{:S(2)}, u32[]{:S(2)}) collective-permute-start(f32[31,32,1]{2,1,0:T(8,128)S(1)} %get-tuple-element.1195), channel_id=1, source_target_pairs={{0,8},{8,0},{1,9},{9,1},{2,10},{10,2},{3,11},{11,3},{4,12},{12,4},... | collective-permute-start | bytes 11912 | tf_op jit(solution)/shard_map/ppermute | solution.py:127
  59.1 48.9 %collective-permute-start.9 = (f32[31,32,1]{2,1,0:T(8,128)S(1)}, f32[31,32,1]{2,1,0:T(8,128)S(1)}, u32[]{:S(2)}, u32[]{:S(2)}) collective-permute-start(f32[31,32,1]{2,1,0:T(8,128)S(1)} %get-tuple-element.1193), channel_id=1, source_target_pairs={{0,8},{8,0},{1,9},{9,1},{2,10},{10,2},{3,11},{11,3},{4,12},{12,4},... | collective-permute-start | bytes 11912 | tf_op jit(solution)/shard_map/ppermute | solution.py:127
  64.9 533.7 %collective-permute-start.22 = (f32[1,514]{1,0:T(1,128)}, f32[1,514]{1,0:T(1,128)}, u32[]{:S(2)}, u32[]{:S(2)}) collective-permute-start(f32[1,514]{1,0:T(1,128)} %pad_maximum_fusion.52), channel_id=1, source_target_pairs={{1,0},{2,1},{3,2},{4,3},{5,4},{6,5},{7,6},{9,8},{10,9},{11,10},{12... | collective-permute-start | bytes 6176 | tf_op jit(solution)/shard_map/ppermute | solution.py:130
  86.2 24.9 %collective-permute-start.8 = (f32[31,1,514]{2,1,0:T(1,128)S(1)}, f32[31,1,514]{2,1,0:T(1,128)S(1)}, u32[]{:S(2)}, u32[]{:S(2)}) collective-permute-start(f32[31,1,514]{2,1,0:T(1,128)S(1)} %get-tuple-element.1183), channel_id=1, source_target_pairs={{0,1},{1,2},{2,3},{3,4},{4,5},{5,6},{6,7},{8,9},{9,10},{10,11},{11... | collective-permute-start | bytes 191216 | tf_op jit(solution)/shard_map/ppermute | solution.py:129
  98.2 19.8 %collective-permute-start.15 = (f32[31,1,514]{2,1,0:T(1,128)S(1)}, f32[31,1,514]{2,1,0:T(1,128)S(1)}, u32[]{:S(2)}, u32[]{:S(2)}) collective-permute-start(f32[31,1,514]{2,1,0:T(1,128)S(1)} %get-tuple-element.1188), channel_id=1, source_target_pairs={{0,1},{1,2},{2,3},{3,4},{4,5},{5,6},{6,7},{8,9},{9,10},{10,11},{11... | collective-permute-start | bytes 191216 | tf_op jit(solution)/shard_map/ppermute | solution.py:129
  100.5 19.4 %collective-permute-start.16 = (f32[31,1,514]{2,1,0:T(1,128)S(1)}, f32[31,1,514]{2,1,0:T(1,128)S(1)}, u32[]{:S(2)}, u32[]{:S(2)}) collective-permute-start(f32[31,1,514]{2,1,0:T(1,128)S(1)} %get-tuple-element.1189), channel_id=1, source_target_pairs={{1,0},{2,1},{3,2},{4,3},{5,4},{6,5},{7,6},{9,8},{10,9},{11,10},{12... | collective-permute-start | bytes 191216 | tf_op jit(solution)/shard_map/ppermute | solution.py:130
  109.1 124.8 %collective-permute-start.19 = (f32[31,1,514]{2,1,0:T(1,128)}, f32[31,1,514]{2,1,0:T(1,128)}, u32[]{:S(2)}, u32[]{:S(2)}) collective-permute-start(f32[31,1,514]{2,1,0:T(1,128)} %get-tuple-element.1186), channel_id=1, source_target_pairs={{0,1},{1,2},{2,3},{3,4},{4,5},{5,6},{6,7},{8,9},{9,10},{10,11},{11... | collective-permute-start | bytes 191216 | tf_op jit(solution)/shard_map/ppermute | solution.py:129
  113.5 124.5 %collective-permute-start.20 = (f32[31,1,514]{2,1,0:T(1,128)}, f32[31,1,514]{2,1,0:T(1,128)}, u32[]{:S(2)}, u32[]{:S(2)}) collective-permute-start(f32[31,1,514]{2,1,0:T(1,128)} %get-tuple-element.1187), channel_id=1, source_target_pairs={{1,0},{2,1},{3,2},{4,3},{5,4},{6,5},{7,6},{9,8},{10,9},{11,10},{12... | collective-permute-start | bytes 191216 | tf_op jit(solution)/shard_map/ppermute | solution.py:130
  118.0 248.9 %collective-permute-start.11 = (f32[31,1,514]{2,1,0:T(1,128)}, f32[31,1,514]{2,1,0:T(1,128)}, u32[]{:S(2)}, u32[]{:S(2)}) collective-permute-start(f32[31,1,514]{2,1,0:T(1,128)} %get-tuple-element.1184), channel_id=1, source_target_pairs={{1,0},{2,1},{3,2},{4,3},{5,4},{6,5},{7,6},{9,8},{10,9},{11,10},{12... | collective-permute-start | bytes 191216 | tf_op jit(solution)/shard_map/ppermute | solution.py:130
  231.5 137.5 %collective-permute-start.12 = (f32[31,1,514]{2,1,0:T(1,128)}, f32[31,1,514]{2,1,0:T(1,128)}, u32[]{:S(2)}, u32[]{:S(2)}) collective-permute-start(f32[31,1,514]{2,1,0:T(1,128)} %get-tuple-element.1185), channel_id=1, source_target_pairs={{0,1},{1,2},{2,3},{3,4},{4,5},{5,6},{6,7},{8,9},{9,10},{10,11},{11... | collective-permute-start | bytes 191216 | tf_op jit(solution)/shard_map/ppermute | solution.py:129
  233.9 249.7 %collective-permute-start.25 = (f32[31,1,514]{2,1,0:T(1,128)}, f32[31,1,514]{2,1,0:T(1,128)}, u32[]{:S(2)}, u32[]{:S(2)}) collective-permute-start(f32[31,1,514]{2,1,0:T(1,128)} %get-tuple-element.1182), channel_id=1, source_target_pairs={{1,0},{2,1},{3,2},{4,3},{5,4},{6,5},{7,6},{9,8},{10,9},{11,10},{12... | collective-permute-start | bytes 191216 | tf_op jit(solution)/shard_map/ppermute | solution.py:130
  637.6 5.9 collective-permute-start.3
  682.4 5.9 collective-permute-start.3
  (169 other events, 1740.2 us)
where the time goes:
time: 1070 us; the launch traced here: 1060 us
  other arithmetic  535 us (50%)
  starting transfers between devices  235 us (22%)
  waiting for transfers between devices  233 us (22%)
  local copies, waits for them, and re-layouts  51.3 us (5%)
    dynamic_update_slice x248, other arithmetic, tri_solve(): lax.scan(down, start, (low_links, up_links, right_side))  397 us
    ppermute x35, waiting for transfers between devices, exchange(): from_south = lax.ppermute(wide[..., -1:, :], 'row', north_moves)  85.2 us
    ppermute x35, starting transfers between devices, exchange(): from_south = lax.ppermute(wide[..., -1:, :], 'row', north_moves)  83.6 us
    ppermute x36, waiting for transfers between devices, exchange(): from_east = lax.ppermute(field[..., :1], 'col', west_moves)  77.5 us
    ppermute x36, starting transfers between devices, exchange(): from_north = lax.ppermute(wide[..., :1, :], 'row', south_moves)  77.4 us
    ppermute x36, waiting for transfers between devices, exchange(): from_west = lax.ppermute(field[..., -1:], 'col', east_moves)  69.7 us
    ppermute x36, starting transfers between devices, exchange(): from_east = lax.ppermute(field[..., :1], 'col', west_moves)  37.8 us
    ppermute x36, starting transfers between devices, exchange(): from_west = lax.ppermute(field[..., -1:], 'col', east_moves)  36.4 us
  transfers between devices with their start and end apart: 143, of which 95 were waited for; matrix products, arithmetic and copies ran while one was open for 49% of the time, Pallas kernels for 0%

commit v1 on v0

v1 whole, which is shorter than its diff:
```python
import functools

import jax
import jax.numpy as jnp
from jax import lax
from jax.experimental import pallas as pl
from jax.experimental.pallas import tpu as pltpu
from jax.sharding import PartitionSpec as P

TIME_STEP = 1.0
GRAVITY = 16.0
BC_GRAVITY = 4.0
EXPAND_T = 0.2
CONTRACT_S = 0.6
CORIO_F0 = 0.4
CORIO_BETA = 0.4
VISC_R = 2.0
DIFF_R = 0.5

MESH = pl.DeviceIdType.MESH
F32 = jnp.float32

SUB = 8
LANE = 128
ZERO = 0.0
ONE = 1.0
NL = 31
NR = 32
NT = 4
RO = 8
WO = 40
WR = 112
N_COPY = 25
VMEM_MAIN = 40 * 1024 * 1024
VMEM_FINISH = 12 * 1024 * 1024


def factors(strength):
    inner, last = [], []
    before = ZERO
    for level in range(NL):
        low = ZERO if level == 0 else strength
        inner.append(strength / (ONE + low + strength - low * before))
        last.append(strength / (ONE + low - low * before))
        before = inner[-1]
    return inner, last


VISC_IN, VISC_END = factors(VISC_R)
DIFF_IN, DIFF_END = factors(DIFF_R)


def lanes():
    return lax.broadcasted_iota(jnp.int32, (SUB, LANE), 1)


def west_of(own, left):
    return pltpu.roll(jnp.where(lanes() == 127, left, own), 1, 1)


def east_of(own, right):
    return pltpu.roll(jnp.where(lanes() == 0, right, own), 127, 1)


def corio(first, total_rows):
    pos = (first + lax.broadcasted_iota(jnp.int32, (SUB, LANE), 0)).astype(F32)
    fu = CORIO_F0 + CORIO_BETA * ((pos + 0.5) / total_rows - 0.5)
    fv = CORIO_F0 + CORIO_BETA * ((pos + ONE) / total_rows - 0.5)
    return fu, fv


def ocean_kernel(n_row, n_sub,
                 u_in, v_in, t_in, s_in, eta_in, tu_in, tv_in, dep_in, cnt_in,
                 us_o, vs_o, tn_o, sn_o, wide, abuf, lu_o, lv_o, hu_s, hv_s, mu_s, mv_s,
                 ub, vb, tb, sb, pb, wsend, cnt_i, pk_s, pk_r, asend,
                 in_sem, w_sem, send, recv):
    row = lax.axis_index('row')
    col = lax.axis_index('col')
    ocol = 1 - col
    has_s = row > 0
    has_n = row < n_row - 1
    dtb = TIME_STEP / n_sub
    total_rows = float(n_row * NR)

    def dev(step, c):
        return {'row': row + step, 'col': c}

    def remote(idx, src, dst, device):
        return pltpu.make_async_remote_copy(src, dst, send.at[idx], recv.at[idx], device_id=device, device_id_type=MESH)

    fields = ((u_in, ub), (v_in, vb), (t_in, tb), (s_in, sb))
    loads = {}
    for f in (0, 1, 2, 3):
        for t in (0, 3, 1, 2):
            src, dst = fields[f]
            loads[f, t] = pltpu.make_async_copy(src.at[:, :, pl.ds(LANE * t, LANE)], dst.at[t + 1, :, pl.ds(RO, NR), :], in_sem.at[f * 4 + t])
    wloads = {}
    for f, src in enumerate((eta_in, tu_in, tv_in, dep_in, cnt_in)):
        for t in range(NT):
            dst = wide.at[f, t, pl.ds(WO, NR), :] if f < 4 else cnt_i.at[t]
            wloads[f, t] = pltpu.make_async_copy(src.at[:, pl.ds(LANE * t, LANE)], dst, w_sem.at[f * 4 + t])
    for f in (4, 3, 0, 1, 2):
        for t in range(NT):
            wloads[f, t].start()
    for f in (0, 1, 2, 3):
        for t in (0, 3, 1, 2):
            loads[f, t].start()

    barrier = pltpu.get_barrier_semaphore()
    pl.semaphore_signal(barrier, inc=1, device_id=dev(0, ocol), device_id_type=MESH)

    @pl.when(has_n)
    def _():
        for c in (col, ocol):
            pl.semaphore_signal(barrier, inc=1, device_id=dev(1, c), device_id_type=MESH)

    @pl.when(has_s)
    def _():
        for c in (col, ocol):
            pl.semaphore_signal(barrier, inc=1, device_id=dev(-1, c), device_id_type=MESH)

    zero8 = jnp.zeros((SUB, LANE), F32)

    def fill(start3, start2, n2):
        def body3(i, _):
            t = i // NL
            k = lax.rem(i, NL)
            for buf in (ub, vb, tb, sb):
                buf[t, k, pl.ds(start3, SUB), :] = zero8
            return 0
        lax.fori_loop(0, 6 * NL, body3, 0)

        def body2(i, _):
            for f in range(5):
                for rr in range(n2):
                    wide[f, i, pl.ds(start2 + SUB * rr, SUB), :] = zero8
            for f in range(2):
                for rr in range(n2):
                    abuf[f, i, pl.ds(start2 + SUB * rr, SUB), :] = zero8
            return 0
        lax.fori_loop(0, 5, body2, 0)

    @pl.when(jnp.logical_not(has_s))
    def _():
        fill(0, SUB, 4)

    @pl.when(jnp.logical_not(has_n))
    def _():
        fill(40, 72, 4)

    for f in range(5):
        for t in range(5):
            wide[f, t, pl.ds(0, SUB), :] = zero8
            wide[f, t, pl.ds(104, SUB), :] = zero8

    for f in range(5):
        for t in range(NT):
            wloads[f, t].wait()
    for t in range(NT):
        for j in range(4):
            wide[4, t, pl.ds(WO + SUB * j, SUB), :] = cnt_i[t, pl.ds(SUB * j, SUB), :].astype(F32)
    half = lanes() < 64
    for f in range(5):
        for j in range(4):
            rows = pl.ds(WO + SUB * j, SUB)
            wsend[f, pl.ds(SUB * j, SUB), :] = jnp.where(half, wide[f, 0, rows, :], wide[f, 3, rows, :])

    for f in (0, 1, 2, 3):
        for t in (0, 3, 1, 2):
            loads[f, t].wait()
    bufs = (ub, vb, tb, sb)

    def pack(k, accs):
        out = []
        lane = lanes()
        for f in range(4):
            for e in range(2):
                acc = accs[f * 2 + e]
                for j in range(4):
                    slot = 4 * k + j
                    tile = bufs[f][1 + 3 * e, k, pl.ds(RO + SUB * j, SUB), :]
                    moved = pltpu.roll(tile, slot if e == 0 else slot + 1, 1)
                    acc = jnp.where(lane == slot, moved, acc)
                out.append(acc)
        return tuple(out)

    packed = lax.fori_loop(0, NL, pack, (zero8,) * SUB)
    for i in range(SUB):
        pk_s[i] = packed[i]

    barrier_count = 1 + 2 * has_n.astype(jnp.int32) + 2 * has_s.astype(jnp.int32)
    pl.semaphore_wait(barrier, barrier_count)

    east_w = [
        remote(0, pk_s, pk_r, dev(0, ocol)),
        remote(1, wsend, wide.at[:, 4, pl.ds(WO, NR), :], dev(0, ocol)),
    ]
    own4 = pl.ds(0, NT)
    mid4 = pl.ds(1, NT)

    def rows3(buf, a, b):
        return buf.at[mid4, :, pl.ds(a, 1), :], buf.at[mid4, :, pl.ds(b, 1), :]

    def rows2(f, nf, a, b, n):
        return wide.at[pl.ds(f, nf), own4, pl.ds(a, n), :], wide.at[pl.ds(f, nf), own4, pl.ds(b, n), :]

    to_n = [
        remote(2, *rows2(3, 2, WO + 24, WO - SUB, SUB), dev(1, col)),
        remote(3, *rows3(ub, 39, 7), dev(1, col)),
        remote(4, *rows3(vb, 39, 7), dev(1, col)),
        remote(16, vb.at[1, :, pl.ds(39, 1), :], vb.at[5, :, pl.ds(7, 1), :], dev(1, ocol)),
        remote(5, *rows3(tb, 39, 7), dev(1, col)),
        remote(6, *rows3(sb, 39, 7), dev(1, col)),
        remote(7, *rows2(3, 2, WO, WO - NR, 24), dev(1, col)),
        remote(SUB, *rows2(0, 3, WO, WO - NR, NR), dev(1, col)),
        remote(17, wsend, wide.at[:, 4, pl.ds(WO - NR, NR), :], dev(1, ocol)),
    ]
    to_s = [
        remote(9, *rows2(3, 2, WO, WO + NR, SUB), dev(-1, col)),
        remote(10, *rows3(ub, SUB, 40), dev(-1, col)),
        remote(11, *rows3(vb, SUB, 40), dev(-1, col)),
        remote(18, ub.at[4, :, pl.ds(SUB, 1), :], ub.at[0, :, pl.ds(40, 1), :], dev(-1, ocol)),
        remote(12, *rows3(tb, SUB, 40), dev(-1, col)),
        remote(13, *rows3(sb, SUB, 40), dev(-1, col)),
        remote(14, *rows2(3, 2, WO + SUB, WO + 40, 24), dev(-1, col)),
        remote(15, *rows2(0, 3, WO, WO + NR, NR), dev(-1, col)),
        remote(19, wsend, wide.at[:, 4, pl.ds(WO + NR, NR), :], dev(-1, ocol)),
    ]
    for cp in east_w:
        cp.start()

    @pl.when(has_n)
    def _():
        for cp in to_n:
            cp.start()

    @pl.when(has_s)
    def _():
        for cp in to_s:
            cp.start()

    p_unit = 0.5 * BC_GRAVITY / NL

    def pressure(t, start):
        rows = pl.ds(start, SUB)
        total = zero8
        for k in range(NL):
            part = (p_unit * CONTRACT_S) * sb[t, k, rows, :] - (p_unit * EXPAND_T) * tb[t, k, rows, :]
            here = total + part
            pb[t, k, rows, :] = here
            total = here + part

    def pressure_own(i, _):
        pressure(1 + i // 4, pl.multiple_of(RO + SUB * lax.rem(i, 4), SUB))
        return 0
    lax.fori_loop(0, 16, pressure_own, 0)

    for cp in east_w:
        cp.wait_recv()

    def unpack(k, _):
        for f in range(4):
            for e in range(2):
                got = pk_r[f * 2 + e]
                for j in range(4):
                    slot = 4 * k + j
                    if e == 0:
                        bufs[f][5, k, pl.ds(RO + SUB * j, SUB), :] = pltpu.roll(got, LANE - slot, 1)
                    else:
                        bufs[f][0, k, pl.ds(RO + SUB * j, SUB), :] = pltpu.roll(got, 127 - slot, 1)
        return 0
    lax.fori_loop(0, NL, unpack, 0)

    def pressure_east(i, _):
        pressure(5, pl.multiple_of(RO + SUB * i, SUB))
        return 0
    lax.fori_loop(0, 4, pressure_east, 0)

    def near2d(f, t, j):
        c = wide[f, t, pl.ds(WO + SUB * j, SUB), :]
        e = east_of(c, wide[f, t + 1, pl.ds(WO + SUB * j, SUB), :])
        n = wide[f, t, pl.ds(WO + 1 + SUB * j, SUB), :]
        return c, e, n

    def momentum(lt, j):
        rc, rn, rs = pl.ds(RO + SUB * j, SUB), pl.ds(RO + 1 + SUB * j, SUB), pl.ds(RO - 1 + SUB * j, SUB)
        ro = pl.ds(SUB * j, SUB)
        t = lt + 1
        fu, fv = corio(row * NR + SUB * j, total_rows)
        fu4 = 0.25 * fu
        fv4 = 0.25 * fv
        c0, ce, cn = near2d(4, lt, j)
        lu = jnp.minimum(c0, ce)
        lv = jnp.minimum(c0, cn)
        d0, de, dn = near2d(3, lt, j)
        hu = 0.5 * (d0 + de)
        hv = 0.5 * (d0 + dn)
        lu_o[lt, ro, :] = lu
        lv_o[lt, ro, :] = lv
        hu_s[lt, ro, :] = hu
        hv_s[lt, ro, :] = hv
        yu, yv = zero8, zero8
        su, sv = zero8, zero8
        for k in range(NL):
            u = ub[t, k, rc, :]
            v = vb[t, k, rc, :]
            uw = west_of(u, ub[t - 1, k, rc, :])
            ue = east_of(u, ub[t + 1, k, rc, :])
            un = ub[t, k, rn, :]
            us = ub[t, k, rs, :]
            unw = west_of(un, ub[t - 1, k, rn, :])
            vw = west_of(v, vb[t - 1, k, rc, :])
            vright = vb[t + 1, k, rc, :]
            ve = east_of(v, vright)
            vn = vb[t, k, rn, :]
            vs = vb[t, k, rs, :]
            v2 = v + vs
            v4 = v2 + east_of(v2, vright + vb[t + 1, k, rs, :])
            u4 = (u + uw) + (un + unw)
            p = pb[t, k, rc, :]
            pe = east_of(p, pb[t + 1, k, rc, :])
            pn = pb[t, k, rn, :]
            ustar = u + (v4 * (fu4 - 0.125 * (un - us)) - 0.5 * u * (ue - uw) - (pe - p))
            vstar = v - (u4 * (fv4 + 0.125 * (ve - vw)) + 0.5 * v * (vn - vs) + (pn - p))
            yu = (ustar + yu) * (jnp.where(lu > k + 1, VISC_IN[k], VISC_END[k]) if k < NL - 1 else VISC_END[k])
            yv = (vstar + yv) * (jnp.where(lv > k + 1, VISC_IN[k], VISC_END[k]) if k < NL - 1 else VISC_END[k])
            us_o[lt, k, ro, :] = yu
            vs_o[lt, k, ro, :] = yv
            su = su + jnp.where(lu > k, u, ZERO)
            sv = sv + jnp.where(lv > k, v, ZERO)
        mu, mv = zero8, zero8
        xu, xv = zero8, zero8
        for k in reversed(range(NL)):
            xu = us_o[lt, k, ro, :] + (jnp.where(lu > k + 1, VISC_IN[k] * xu, ZERO) if k < NL - 1 else ZERO)
            xv = vs_o[lt, k, ro, :] + (jnp.where(lv > k + 1, VISC_IN[k] * xv, ZERO) if k < NL - 1 else ZERO)
            outu = (ONE / VISC_R) * xu
            outv = (ONE / VISC_R) * xv
            us_o[lt, k, ro, :] = outu
            vs_o[lt, k, ro, :] = outv
            mu = mu + jnp.where(lu > k, outu, ZERO)
            mv = mv + jnp.where(lv > k, outv, ZERO)
        iu = ONE / jnp.maximum(lu, ONE)
        iv = ONE / jnp.maximum(lv, ONE)
        mu_s[lt, ro, :] = mu * iu
        mv_s[lt, ro, :] = mv * iv
        scale = dtb * dtb / TIME_STEP
        rw = pl.ds(WO + SUB * j, SUB)
        abuf[0, lt, rw, :] = jnp.where(lu > ZERO, scale * hu * ((mu - su) * iu), ZERO)
        abuf[1, lt, rw, :] = jnp.where(lv > ZERO, scale * hv * ((mv - sv) * iv), ZERO)

    def momentum_inner(i, _):
        momentum(lax.rem(i, 4), 1 + i // 4)
        return 0
    lax.fori_loop(0, SUB, momentum_inner, 0)

    @pl.when(has_s)
    def _():
        for cp in (to_n[0], to_n[1], to_n[2], to_n[3]):
            cp.wait_recv()

    @pl.when(has_n)
    def _():
        for cp in (to_s[0], to_s[1], to_s[2], to_s[3], to_s[4], to_s[5]):
            cp.wait_recv()

    def pressure_north(i, _):
        pressure(1 + i, RO + NR)
        return 0
    lax.fori_loop(0, 4, pressure_north, 0)

    def momentum_outer(i, _):
        momentum(lax.rem(i, 4), 3 * (i // 4))
        return 0
    lax.fori_loop(0, SUB, momentum_outer, 0)

    for f in range(2):
        for j in range(4):
            rows = pl.ds(WO + SUB * j, SUB)
            asend[f, pl.ds(SUB * j, SUB), :] = jnp.where(half, abuf[f, 0, rows, :], abuf[f, 3, rows, :])

    def arows(b):
        return abuf.at[:, own4, pl.ds(WO, NR), :], abuf.at[:, own4, pl.ds(b, NR), :]

    force_z = remote(20, asend, abuf.at[:, 4, pl.ds(WO, NR), :], dev(0, ocol))
    force_n = [remote(21, *arows(WO - NR), dev(1, col)), remote(23, asend, abuf.at[:, 4, pl.ds(WO - NR, NR), :], dev(1, ocol))]
    force_s = [remote(22, *arows(WO + NR), dev(-1, col)), remote(24, asend, abuf.at[:, 4, pl.ds(WO + NR, NR), :], dev(-1, ocol))]
    force_z.start()

    @pl.when(has_n)
    def _():
        for cp in force_n:
            cp.start()

    @pl.when(has_s)
    def _():
        for cp in force_s:
            cp.start()

    @pl.when(has_s)
    def _():
        for cp in (to_n[4], to_n[5]):
            cp.wait_recv()

    def tracers(lt, j):
        rc, rn, rs = pl.ds(RO + SUB * j, SUB), pl.ds(RO + 1 + SUB * j, SUB), pl.ds(RO - 1 + SUB * j, SUB)
        ro = pl.ds(SUB * j, SUB)
        t = lt + 1
        rw = pl.ds(WO + SUB * j, SUB)
        c0 = wide[4, lt, rw, :]
        left = lax.rem(lt + 4, 5)
        luw = jnp.minimum(c0, west_of(c0, wide[4, left, rw, :]))
        lvs = jnp.minimum(c0, wide[4, lt, pl.ds(WO - 1 + SUB * j, SUB), :])
        lu = lu_o[lt, ro, :]
        lv = lv_o[lt, ro, :]
        half_dt = 0.5 * TIME_STEP
        yt, ys = zero8, zero8
        for k in range(NL):
            u = ub[t, k, rc, :]
            me = jnp.where(lu > k, half_dt * u, ZERO)
            mw = jnp.where(luw > k, half_dt * west_of(u, ub[t - 1, k, rc, :]), ZERO)
            mn = jnp.where(lv > k, half_dt * vb[t, k, rc, :], ZERO)
            ms = jnp.where(lvs > k, half_dt * vb[t, k, rs, :], ZERO)

            def advect(buf):
                q = buf[t, k, rc, :]
                qe = east_of(q, buf[t + 1, k, rc, :])
                qw = west_of(q, buf[t - 1, k, rc, :])
                qn = buf[t, k, rn, :]
                qs = buf[t, k, rs, :]
                return q - ((me * (q + qe) - mw * (qw + q)) + (mn * (q + qn) - ms * (qs + q)))

            qt = advect(tb)
            qs_ = advect(sb)
            fac = jnp.where(c0 > k + 1, DIFF_IN[k], DIFF_END[k]) if k < NL - 1 else DIFF_END[k]
            yt = jnp.where(c0 > k, (qt + yt) * fac, DIFF_R * qt)
            ys = jnp.where(c0 > k, (qs_ + ys) * fac, DIFF_R * qs_)
            tn_o[lt, k, ro, :] = yt
            sn_o[lt, k, ro, :] = ys
        xt, xs_ = zero8, zero8
        for k in reversed(range(NL)):
            xt = tn_o[lt, k, ro, :] + (jnp.where(c0 > k + 1, DIFF_IN[k] * xt, ZERO) if k < NL - 1 else ZERO)
            xs_ = sn_o[lt, k, ro, :] + (jnp.where(c0 > k + 1, DIFF_IN[k] * xs_, ZERO) if k < NL - 1 else ZERO)
            tn_o[lt, k, ro, :] = (ONE / DIFF_R) * xt
            sn_o[lt, k, ro, :] = (ONE / DIFF_R) * xs_

    def tracers_all(i, _):
        tracers(lax.rem(i, 4), i // 4)
        return 0
    lax.fori_loop(0, 16, tracers_all, 0)

    @pl.when(has_s)
    def _():
        for cp in (to_n[6], to_n[7], to_n[SUB]):
            cp.wait_recv()

    @pl.when(has_n)
    def _():
        for cp in (to_s[6], to_s[7], to_s[SUB]):
            cp.wait_recv()

    force_z.wait_recv()

    @pl.when(has_s)
    def _():
        for cp in force_n:
            cp.wait_recv()

    @pl.when(has_n)
    def _():
        for cp in force_s:
            cp.wait_recv()

    for cp in east_w + [force_z]:
        cp.wait_send()

    @pl.when(has_n)
    def _():
        for cp in to_n + force_n:
            cp.wait_send()

    @pl.when(has_s)
    def _():
        for cp in to_s + force_s:
            cp.wait_send()


def finish_kernel(n_row, n_sub, w_ref,
                  us, vs, tn, sn, wide, abuf, lu, lv, hu_s, hv_s, mu_s, mv_s,
                  eta_o, tu_o, tv_o, u_o, v_o, t_o, s_o,
                  bu, bv, cfu, cfv, mku, mkv, tu, tv, xs, acu, acv, cu, cv, flat_b, ubuf, vbuf, sem):
    row = lax.axis_index('row')
    dtb = TIME_STEP / n_sub
    total_rows = float(n_row * NR)
    zero8 = jnp.zeros((SUB, LANE), F32)
    copies = []

    def put(src, dst):
        cp = pltpu.make_async_copy(src, dst, sem.at[len(copies)])
        cp.start()
        copies.append(cp)

    for src, dst in ((tn, t_o), (sn, s_o)):
        for t in range(NT):
            put(src.at[t], dst.at[:, :, pl.ds(LANE * t, LANE)])

    def setup(i, _):
        base = SUB + SUB * i
        rows = pl.ds(base, SUB)
        rown = pl.ds(base + 1, SUB)
        fu, fv = corio(row * NR + SUB * i - NR, total_rows)
        for t in range(5):
            right = (t + 1) % 5
            c0 = wide[4, t, rows, :]
            wet_u = (jnp.minimum(c0, east_of(c0, wide[4, right, rows, :])) > ZERO).astype(F32)
            wet_v = (jnp.minimum(c0, wide[4, t, rown, :]) > ZERO).astype(F32)
            d0 = wide[3, t, rows, :]
            scale = dtb * dtb * GRAVITY * 0.5
            bu[t, rows, :] = wet_u * (scale * (d0 + east_of(d0, wide[3, right, rows, :])))
            bv[t, rows, :] = wet_v * (scale * (d0 + wide[3, t, rown, :]))
            cfu[t, rows, :] = wet_u * ((0.25 * dtb) * fu)
            cfv[t, rows, :] = wet_v * ((0.25 * dtb) * fv)
            mku[t, rows, :] = wet_u
            mkv[t, rows, :] = wet_v
            tu[0, t, rows, :] = dtb * wide[1, t, rows, :]
            tv[0, t, rows, :] = dtb * wide[2, t, rows, :]
        return 0
    lax.fori_loop(0, 12, setup, 0)
    for t in range(5):
        for a in (0, 1):
            for start in (0, 104):
                tu[a, t, pl.ds(start, SUB), :] = zero8
                tv[a, t, pl.ds(start, SUB), :] = zero8
        for i in range(2):
            xs[t, pl.ds(104 * i, SUB), :] = zero8
    for i in range(13):
        for t in range(5):
            tu[1, t, pl.ds(SUB * i + SUB, SUB), :] = zero8
            tv[1, t, pl.ds(SUB * i + SUB, SUB), :] = zero8
            xs[t, pl.ds(SUB * i + SUB, SUB), :] = zero8
    for t in range(NT):
        for j in range(4):
            acu[t, pl.ds(SUB * j, SUB), :] = zero8
            acv[t, pl.ds(SUB * j, SUB), :] = zero8

    def subcycle(n, cur, lo, hi, first=False):
        nxt = 1 - cur
        weight = w_ref[n] * (ONE / dtb)
        for i in range(lo, hi):
            rows = pl.ds(SUB + SUB * i, SUB)
            rows_s = pl.ds(7 + SUB * i, SUB)
            us = [tu[cur, t, rows, :] for t in range(5)]
            for t in range(5):
                uw = west_of(us[t], us[(t + 4) % 5])
                xs[t, rows, :] = us[t] + uw
                wide[0, t, rows, :] = wide[0, t, rows, :] - ((us[t] - uw) + (tv[cur, t, rows, :] - tv[cur, t, rows_s, :]))
        for i in range(lo, hi):
            rows = pl.ds(SUB + SUB * i, SUB)
            rows_s = pl.ds(7 + SUB * i, SUB)
            rows_n = pl.ds(9 + SUB * i, SUB)
            es = [wide[0, t, rows, :] for t in range(5)]
            v0 = [tv[cur, t, rows, :] for t in range(5)]
            v2 = [v0[t] + tv[cur, t, rows_s, :] for t in range(5)]
            for t in range(5):
                right = (t + 1) % 5
                v4 = v2[t] + east_of(v2[t], v2[right])
                slope_u = east_of(es[t], es[right]) - es[t]
                slope_v = wide[0, t, rows_n, :] - es[t]
                u4 = xs[t, rows, :] + xs[t, rows_n, :]
                u_old = tu[cur, t, rows, :]
                v_old = v0[t]
                if first:
                    u_old = mku[t, rows, :] * u_old
                    v_old = mkv[t, rows, :] * v_old
                u_new = (u_old + abuf[0, t, rows, :]) + (cfu[t, rows, :] * v4 - bu[t, rows, :] * slope_u)
                v_new = (v_old + abuf[1, t, rows, :]) - (cfv[t, rows, :] * u4 + bv[t, rows, :] * slope_v)
                tu[nxt, t, rows, :] = u_new
                tv[nxt, t, rows, :] = v_new
                if 4 <= i < SUB and t < NT:
                    ro = pl.ds(SUB * (i - 4), SUB)
                    acu[t, ro, :] += weight * u_new
                    acv[t, ro, :] += weight * v_new

    def pairs(first_n, count, lo, hi):
        def body(i, _):
            n = first_n + 2 * i
            subcycle(n, 0, lo, hi)
            subcycle(n + 1, 1, lo, hi)
            return 0
        lax.fori_loop(0, count, body, 0)

    subcycle(0, 0, 0, 12, first=True)
    subcycle(1, 1, 0, 12)
    pairs(2, 2, 0, 12)
    pairs(6, 4, 1, 11)
    pairs(14, 4, 2, 10)
    pairs(22, 4, 3, 9)

    for t in range(NT):
        for j in range(4):
            rw = pl.ds(WO + SUB * j, SUB)
            ro = pl.ds(SUB * j, SUB)
            flat_b[0, t, ro, :] = wide[0, t, rw, :]
            flat_b[1, t, ro, :] = (ONE / dtb) * tu[0, t, rw, :]
            flat_b[2, t, ro, :] = (ONE / dtb) * tv[0, t, rw, :]
            cu[t, ro, :] = acu[t, ro, :] / hu_s[t, ro, :] - mu_s[t, ro, :]
            hv = hv_s[t, ro, :]
            cv[t, ro, :] = acv[t, ro, :] / hv - mv_s[t, ro, :]

    for f, dst in enumerate((eta_o, tu_o, tv_o)):
        for t in range(NT):
            put(flat_b.at[f, t], dst.at[:, pl.ds(LANE * t, LANE)])
    for lev, cor, src, buf, dst in ((lu, cu, us, ubuf, u_o), (lv, cv, vs, vbuf, v_o)):
        for t in range(NT):
            for j in range(4):
                ro = pl.ds(SUB * j, SUB)
                count = lev[t, ro, :]
                shift = cor[t, ro, :]
                for k in range(NL):
                    buf[t, k, ro, :] = jnp.where(count > k, src[t, k, ro, :] + shift, ZERO)
            put(buf.at[t], dst.at[:, :, pl.ds(LANE * t, LANE)])
    for cp in copies:
        cp.wait()


def solution(mesh):
    n_row = mesh.shape['row']

    def step(vel_u, vel_v, temperature, salinity, surf_eta, trans_u, trans_v, bottom_depth, level_count, avg_weights):
        n_sub = avg_weights.shape[0]
        hbm = pl.BlockSpec(memory_space=pltpu.HBM)
        vmem = pl.BlockSpec(memory_space=pltpu.VMEM)
        smem = pl.BlockSpec(memory_space=pltpu.SMEM)
        cube_v = pltpu.VMEM((NT, NL, NR, LANE), F32)
        flat_v = pltpu.VMEM((NT, NR, LANE), F32)
        pad3 = pltpu.VMEM((6, NL, 48, LANE), F32)
        wide1 = pltpu.VMEM((5, WR, LANE), F32)
        wide_v = pltpu.VMEM((5, 5, WR, LANE), F32)
        force_v = pltpu.VMEM((2, 5, WR, LANE), F32)
        sems = pltpu.SemaphoreType.DMA
        outs = [cube_v] * 4 + [wide_v, force_v] + [flat_v] * 6
        mids = pl.pallas_call(
            functools.partial(ocean_kernel, n_row, n_sub),
            out_shape=outs,
            in_specs=[hbm] * 9,
            out_specs=[vmem] * len(outs),
            scratch_shapes=[pad3] * 5 + [
                pltpu.VMEM((5, NR, LANE), F32),
                pltpu.VMEM((NT, NR, LANE), jnp.int32),
                pltpu.VMEM((SUB, SUB, LANE), F32),
                pltpu.VMEM((SUB, SUB, LANE), F32),
                pltpu.VMEM((2, NR, LANE), F32),
                sems((16,)), sems((20,)), sems((N_COPY,)), sems((N_COPY,)),
            ],
            compiler_params=pltpu.CompilerParams(collective_id=0, has_side_effects=True, vmem_limit_bytes=VMEM_MAIN),
            name='ocean',
        )(*[pltpu.with_memory_space_constraint(x, pltpu.HBM) for x in (vel_u, vel_v, temperature, salinity, surf_eta, trans_u, trans_v, bottom_depth, level_count)])
        cube = jax.ShapeDtypeStruct((NL, NR, NT * LANE), F32)
        flat = jax.ShapeDtypeStruct((NR, NT * LANE), F32)
        return pl.pallas_call(
            functools.partial(finish_kernel, n_row, n_sub),
            out_shape=[flat] * 3 + [cube] * 4,
            in_specs=[smem] + [vmem] * len(outs),
            out_specs=[hbm] * 7,
            scratch_shapes=[wide1] * 6 + [force_v, force_v, wide1] + [flat_v] * 4 + [pltpu.VMEM((3, NT, NR, LANE), F32), cube_v, cube_v, sems((28,))],
            compiler_params=pltpu.CompilerParams(vmem_limit_bytes=VMEM_FINISH),
            name='finish',
        )(avg_weights, *mids)

    cube = P(None, 'row', 'col')
    flat = P('row', 'col')
    return jax.shard_map(step, mesh=mesh, in_specs=(cube, cube, cube, cube, flat, flat, flat, flat, flat, P()), out_specs=(flat, flat, flat, cube, cube, cube, cube), check_vma=False)
```

time: 1070 us -> 44 us (0.04)
  the two profiles are of different devices: /device:TPU:4 before, /device:TPU:0 now
where the time goes in v1:
time: 44 us; the launch traced here: 43.9 us
  Pallas kernels  43.2 us (98%)
  between operations  0.66 us (2%)
    pallas_call x1, Pallas kernels, step(): pl.pallas_call(functools.partial(ocean_kernel, n_row, n_sub), out_shape=o...  31.1 us
    pallas_call x1, Pallas kernels, step(): pl.pallas_call(functools.partial(finish_kernel, n_row, n_sub), out_shape=...  12.1 us

profile of v1, /device:TPU:0, one launch (start us, length us, event | category | flops | bytes accessed | tf_op | source)
XLA Modules:
  0.0 43.9 jit_solution(7673583507909110877)
XLA Ops:
  0.6 0.0 copy-start
  0.6 31.1 %ocean.1 = (f32[4,31,32,128]{3,2,1,0:T(8,128)S(1)}, f32[4,31,32,128]{3,2,1,0:T(8,128)S(1)}, f32[4,31,32,128]{3,2,1,0:T(8,128)S(1)}, f32[4,31,32,128]{3,2,1,0:T(8...) custom-call(f32[31,32,512]{2,1,0:T(8,128)} %u_in.1, ...), custom_call_target="tpu_custom_call" | custom-call | tf_op jit(solution)/shard_map/ocean/pallas_call | solution.py:641
  31.8 0.0 copy-done
  31.8 12.1 %finish.1 = (f32[32,512]{1,0:T(8,128)}, f32[32,512]{1,0:T(8,128)}, f32[32,512]{1,0:T(8,128)}, f32[31,32,512]{2,1,0:T(8,128)}, f32[31,32,512]{2,1,0:T(8,128)}, /*...) custom-call(f32[30]{0:T(128)S(1)} %copy-done, f32[4,31,32,128]{3,2,1,0:T(8,128)S(1)} %get-tuple-element.19.us, ...), custom_call_target="tpu_custom_call" | custom-call | tf_op jit(solution)/shard_map/finish/pallas_call | solution.py:659
Async XLA Ops:
  0.6 31.1 %copy-start = (f32[30]{0:T(128)S(1)}, f32[30]{0:T(128)}, u32[]{:S(2)}) copy-start(f32[30]{0:T(128)} %w_ref.1) | copy-start | bytes 364

commit v2 on v1

--- a/solution.py
+++ b/solution.py
@@ -30,7 +30,8 @@
 RO = 8
 WO = 40
 WR = 112
-N_COPY = 25
+N_COPY = 32
+NH = 30
 VMEM_MAIN = 40 * 1024 * 1024
 VMEM_FINISH = 12 * 1024 * 1024
 
@@ -72,7 +73,7 @@
 def ocean_kernel(n_row, n_sub,
                  u_in, v_in, t_in, s_in, eta_in, tu_in, tv_in, dep_in, cnt_in,
                  us_o, vs_o, tn_o, sn_o, wide, abuf, lu_o, lv_o, hu_s, hv_s, mu_s, mv_s,
-                 ub, vb, tb, sb, pb, wsend, cnt_i, pk_s, pk_r, asend,
+                 fb, pb, cnt, wsend, cnt_i, pk_s, pk_r, asend,
                  in_sem, w_sem, send, recv):
     row = lax.axis_index('row')
     col = lax.axis_index('col')
@@ -81,30 +82,54 @@
     has_n = row < n_row - 1
     dtb = TIME_STEP / n_sub
     total_rows = float(n_row * NR)
+    used = []
+    ub, vb, tb, sb = (fb.at[f] for f in range(4))
+    zero8 = jnp.zeros((SUB, LANE), F32)
 
     def dev(step, c):
         return {'row': row + step, 'col': c}
 
-    def remote(idx, src, dst, device):
+    def remote(src, dst, device):
+        used.append(0)
+        idx = len(used) - 1
         return pltpu.make_async_remote_copy(src, dst, send.at[idx], recv.at[idx], device_id=device, device_id_type=MESH)
 
-    fields = ((u_in, ub), (v_in, vb), (t_in, tb), (s_in, sb))
-    loads = {}
-    for f in (0, 1, 2, 3):
-        for t in (0, 3, 1, 2):
-            src, dst = fields[f]
-            loads[f, t] = pltpu.make_async_copy(src.at[:, :, pl.ds(LANE * t, LANE)], dst.at[t + 1, :, pl.ds(RO, NR), :], in_sem.at[f * 4 + t])
-    wloads = {}
-    for f, src in enumerate((eta_in, tu_in, tv_in, dep_in, cnt_in)):
+    def start(copies):
+        for cp in copies:
+            cp.start()
+
+    def both(south, north, action):
+        @pl.when(has_s)
+        def _():
+            for cp in south:
+                action(cp)
+
+        @pl.when(has_n)
+        def _():
+            for cp in north:
+                action(cp)
+
+    def arrived(south_from, north_from):
+        both(south_from, north_from, lambda cp: cp.wait_recv())
+
+    wloads, loads = {}, {}
+    for f, src in enumerate((eta_in, tv_in, tu_in, dep_in, cnt_in)):
         for t in range(NT):
             dst = wide.at[f, t, pl.ds(WO, NR), :] if f < 4 else cnt_i.at[t]
-            wloads[f, t] = pltpu.make_async_copy(src.at[:, pl.ds(LANE * t, LANE)], dst, w_sem.at[f * 4 + t])
-    for f in (4, 3, 0, 1, 2):
+            wloads[f, t] = pltpu.make_async_copy(src.at[:, pl.ds(LANE * t, LANE)], dst, w_sem.at[f * NT + t])
+    for f, src in enumerate((u_in, v_in, t_in, s_in)):
         for t in range(NT):
-            wloads[f, t].start()
-    for f in (0, 1, 2, 3):
-        for t in (0, 3, 1, 2):
-            loads[f, t].start()
+            loads[f, t] = pltpu.make_async_copy(src.at[:, :, pl.ds(LANE * t, LANE)], fb.at[f, t + 1, :, pl.ds(RO, NR), :], in_sem.at[f * NT + t])
+    start(wloads.values())
+    order = [(f, t) for f in range(4) for t in (0, 3)] + [(f, t) for f in (0, 1, 2, 3) for t in (1, 2)]
+    start([loads[key] for key in order])
+
+    for i in range(5):
+        for rr in (0, SUB, WR - 2 * SUB, WR - SUB):
+            for f in range(4):
+                wide[f, i, pl.ds(rr, SUB), :] = zero8
+            for f in range(2):
+                abuf[f, i, pl.ds(rr, SUB), :] = zero8
 
     barrier = pltpu.get_barrier_semaphore()
     pl.semaphore_signal(barrier, inc=1, device_id=dev(0, ocol), device_id_type=MESH)
@@ -119,125 +144,112 @@
         for c in (col, ocol):
             pl.semaphore_signal(barrier, inc=1, device_id=dev(-1, c), device_id_type=MESH)
 
-    zero8 = jnp.zeros((SUB, LANE), F32)
-
-    def fill(start3, start2, n2):
-        def body3(i, _):
-            t = i // NL
-            k = lax.rem(i, NL)
-            for buf in (ub, vb, tb, sb):
-                buf[t, k, pl.ds(start3, SUB), :] = zero8
+    def fill(first3, first2):
+        def body(i, _):
+            for f in range(4):
+                fb[f, i, :, pl.ds(first3, SUB), :] = jnp.zeros((NL, SUB, LANE), F32)
             return 0
-        lax.fori_loop(0, 6 * NL, body3, 0)
-
-        def body2(i, _):
-            for f in range(5):
-                for rr in range(n2):
-                    wide[f, i, pl.ds(start2 + SUB * rr, SUB), :] = zero8
+        lax.fori_loop(0, 6, body, 0)
+        for i in range(5):
+            for f in range(4):
+                wide[f, i, pl.ds(first2, NR), :] = jnp.zeros((NR, LANE), F32)
             for f in range(2):
-                for rr in range(n2):
-                    abuf[f, i, pl.ds(start2 + SUB * rr, SUB), :] = zero8
-            return 0
-        lax.fori_loop(0, 5, body2, 0)
+                abuf[f, i, pl.ds(first2, NR), :] = jnp.zeros((NR, LANE), F32)
+            cnt[i, pl.ds(first3, SUB), :] = zero8
 
     @pl.when(jnp.logical_not(has_s))
     def _():
-        fill(0, SUB, 4)
+        fill(0, WO - NR)
 
     @pl.when(jnp.logical_not(has_n))
     def _():
-        fill(40, 72, 4)
-
-    for f in range(5):
-        for t in range(5):
-            wide[f, t, pl.ds(0, SUB), :] = zero8
-            wide[f, t, pl.ds(104, SUB), :] = zero8
-
-    for f in range(5):
-        for t in range(NT):
-            wloads[f, t].wait()
+        fill(RO + NR, WO + NR)
+
+    for cp in wloads.values():
+        cp.wait()
     for t in range(NT):
-        for j in range(4):
-            wide[4, t, pl.ds(WO + SUB * j, SUB), :] = cnt_i[t, pl.ds(SUB * j, SUB), :].astype(F32)
-    half = lanes() < 64
-    for f in range(5):
-        for j in range(4):
-            rows = pl.ds(WO + SUB * j, SUB)
-            wsend[f, pl.ds(SUB * j, SUB), :] = jnp.where(half, wide[f, 0, rows, :], wide[f, 3, rows, :])
-
-    for f in (0, 1, 2, 3):
+        cnt[t, pl.ds(RO, NR), :] = cnt_i[t].astype(F32)
+    lane = lanes()
+    outer = lane < LANE // 2
+    middle = jnp.logical_and(lane >= NR, lane < LANE - NR)
+
+    def edges(buf, f, first):
+        rows = pl.ds(first, SUB)
+        return jnp.where(outer, buf[f, 0, rows, :], buf[f, 3, rows, :])
+
+    def paired(buf, f, g, first):
+        return jnp.where(middle, pltpu.roll(edges(buf, g, first), LANE // 2, 1), edges(buf, f, first))
+
+    for j in range(4):
+        mine = pl.ds(SUB * j, SUB)
+        first = WO + SUB * j
+        for f in range(2):
+            wsend[f, mine, :] = paired(wide, f, f + 2, first)
+        own = pl.ds(RO + SUB * j, SUB)
+        wsend[2, mine, :] = jnp.where(outer, cnt[0, own, :], cnt[3, own, :])
+
+    barrier_count = 1 + 2 * has_n.astype(jnp.int32) + 2 * has_s.astype(jnp.int32)
+    pl.semaphore_wait(barrier, barrier_count)
+
+    own4 = pl.ds(0, NT)
+    mid4 = pl.ds(1, NT)
+    two = pl.ds(0, 2)
+    top, low, north, south = RO + NR - 1, RO, RO + NR, RO - 1
+    n_src, n_dst, s_src, s_dst = WO + NR - NH, WO - NH, WO, WO + NR
+
+    def rows3(f, a, b, d):
+        return remote(fb.at[f, mid4, :, pl.ds(a, 1), :], fb.at[f, mid4, :, pl.ds(b, 1), :], dev(d, col))
+
+    def rows2(buf, f, nf, a, b, d):
+        return remote(buf.at[pl.ds(f, nf), own4, pl.ds(a, NH), :], buf.at[pl.ds(f, nf), own4, pl.ds(b, NH), :], dev(d, col))
+
+    def row1(a, b, d):
+        return remote(cnt.at[own4, pl.ds(a, 1), :], cnt.at[own4, pl.ds(b, 1), :], dev(d, col))
+
+    def corner(a, b, d):
+        return remote(wsend.at[two, pl.ds(a - WO, NH), :], wide.at[two, 4, pl.ds(b, NH), :], dev(d, ocol))
+
+    z_wide = [
+        remote(wsend.at[2], cnt.at[4, pl.ds(RO, NR), :], dev(0, ocol)),
+        remote(wsend.at[two], wide.at[two, 4, pl.ds(WO, NR), :], dev(0, ocol)),
+    ]
+    n_first = [row1(top, south, 1), rows2(wide, 3, 1, n_src, n_dst, 1)]
+    s_first = [row1(low, north, -1), rows2(wide, 3, 1, s_src, s_dst, -1)]
+    start(z_wide)
+    both(s_first, n_first, lambda cp: cp.start())
+
+    for f in (0, 1):
         for t in (0, 3, 1, 2):
             loads[f, t].wait()
-    bufs = (ub, vb, tb, sb)
-
-    def pack(k, accs):
-        out = []
-        lane = lanes()
-        for f in range(4):
-            for e in range(2):
-                acc = accs[f * 2 + e]
-                for j in range(4):
-                    slot = 4 * k + j
-                    tile = bufs[f][1 + 3 * e, k, pl.ds(RO + SUB * j, SUB), :]
-                    moved = pltpu.roll(tile, slot if e == 0 else slot + 1, 1)
-                    acc = jnp.where(lane == slot, moved, acc)
-                out.append(acc)
-        return tuple(out)
-
-    packed = lax.fori_loop(0, NL, pack, (zero8,) * SUB)
-    for i in range(SUB):
-        pk_s[i] = packed[i]
-
-    barrier_count = 1 + 2 * has_n.astype(jnp.int32) + 2 * has_s.astype(jnp.int32)
-    pl.semaphore_wait(barrier, barrier_count)
-
-    east_w = [
-        remote(0, pk_s, pk_r, dev(0, ocol)),
-        remote(1, wsend, wide.at[:, 4, pl.ds(WO, NR), :], dev(0, ocol)),
-    ]
-    own4 = pl.ds(0, NT)
-    mid4 = pl.ds(1, NT)
-
-    def rows3(buf, a, b):
-        return buf.at[mid4, :, pl.ds(a, 1), :], buf.at[mid4, :, pl.ds(b, 1), :]
-
-    def rows2(f, nf, a, b, n):
-        return wide.at[pl.ds(f, nf), own4, pl.ds(a, n), :], wide.at[pl.ds(f, nf), own4, pl.ds(b, n), :]
-
-    to_n = [
-        remote(2, *rows2(3, 2, WO + 24, WO - SUB, SUB), dev(1, col)),
-        remote(3, *rows3(ub, 39, 7), dev(1, col)),
-        remote(4, *rows3(vb, 39, 7), dev(1, col)),
-        remote(16, vb.at[1, :, pl.ds(39, 1), :], vb.at[5, :, pl.ds(7, 1), :], dev(1, ocol)),
-        remote(5, *rows3(tb, 39, 7), dev(1, col)),
-        remote(6, *rows3(sb, 39, 7), dev(1, col)),
-        remote(7, *rows2(3, 2, WO, WO - NR, 24), dev(1, col)),
-        remote(SUB, *rows2(0, 3, WO, WO - NR, NR), dev(1, col)),
-        remote(17, wsend, wide.at[:, 4, pl.ds(WO - NR, NR), :], dev(1, ocol)),
-    ]
-    to_s = [
-        remote(9, *rows2(3, 2, WO, WO + NR, SUB), dev(-1, col)),
-        remote(10, *rows3(ub, SUB, 40), dev(-1, col)),
-        remote(11, *rows3(vb, SUB, 40), dev(-1, col)),
-        remote(18, ub.at[4, :, pl.ds(SUB, 1), :], ub.at[0, :, pl.ds(40, 1), :], dev(-1, ocol)),
-        remote(12, *rows3(tb, SUB, 40), dev(-1, col)),
-        remote(13, *rows3(sb, SUB, 40), dev(-1, col)),
-        remote(14, *rows2(3, 2, WO + SUB, WO + 40, 24), dev(-1, col)),
-        remote(15, *rows2(0, 3, WO, WO + NR, NR), dev(-1, col)),
-        remote(19, wsend, wide.at[:, 4, pl.ds(WO + NR, NR), :], dev(-1, ocol)),
-    ]
-    for cp in east_w:
-        cp.start()
-
-    @pl.when(has_n)
-    def _():
-        for cp in to_n:
-            cp.start()
-
-    @pl.when(has_s)
-    def _():
-        for cp in to_s:
-            cp.start()
+    n_vel = [rows3(0, top, south, 1), rows3(1, top, south, 1),
+             remote(fb.at[1, 1, :, pl.ds(top, 1), :], fb.at[1, 5, :, pl.ds(south, 1), :], dev(1, ocol))]
+    s_vel = [rows3(0, low, north, -1), rows3(1, low, north, -1),
+             remote(fb.at[0, 4, :, pl.ds(low, 1), :], fb.at[0, 0, :, pl.ds(north, 1), :], dev(-1, ocol))]
+    both(s_vel, n_vel, lambda cp: cp.start())
+    for f in (2, 3):
+        for t in (0, 3, 1, 2):
+            loads[f, t].wait()
+    n_tra = [rows3(2, top, south, 1), rows3(3, top, south, 1)]
+    s_tra = [rows3(2, low, north, -1), rows3(3, low, north, -1)]
+    n_far = [rows2(wide, 0, 3, n_src, n_dst, 1), corner(n_src, n_dst, 1)]
+    s_far = [rows2(wide, 0, 3, s_src, s_dst, -1), corner(s_src, s_dst, -1)]
+    both(s_tra + s_far, n_tra + n_far, lambda cp: cp.start())
+
+    def pack(f, _):
+        here = lanes()
+        east, west = zero8, zero8
+        for k in range(NL):
+            for j in range(4):
+                slot = 4 * k + j
+                rows = pl.ds(RO + SUB * j, SUB)
+                east = jnp.where(here == slot, pltpu.roll(fb[f, 1, k, rows, :], slot, 1) if slot else fb[f, 1, k, rows, :], east)
+                west = jnp.where(here == slot, pltpu.roll(fb[f, 4, k, rows, :], slot + 1, 1), west)
+        pk_s[f, 0] = east
+        pk_s[f, 1] = west
+        return 0
+    lax.fori_loop(0, 4, pack, 0)
+    z_col = remote(pk_s, pk_r, dev(0, ocol))
+    z_col.start()
 
     p_unit = 0.5 * BC_GRAVITY / NL
 
@@ -255,32 +267,11 @@
         return 0
     lax.fori_loop(0, 16, pressure_own, 0)
 
-    for cp in east_w:
-        cp.wait_recv()
-
-    def unpack(k, _):
-        for f in range(4):
-            for e in range(2):
-                got = pk_r[f * 2 + e]
-                for j in range(4):
-                    slot = 4 * k + j
-                    if e == 0:
-                        bufs[f][5, k, pl.ds(RO + SUB * j, SUB), :] = pltpu.roll(got, LANE - slot, 1)
-                    else:
-                        bufs[f][0, k, pl.ds(RO + SUB * j, SUB), :] = pltpu.roll(got, 127 - slot, 1)
-        return 0
-    lax.fori_loop(0, NL, unpack, 0)
-
-    def pressure_east(i, _):
-        pressure(5, pl.multiple_of(RO + SUB * i, SUB))
-        return 0
-    lax.fori_loop(0, 4, pressure_east, 0)
-
-    def near2d(f, t, j):
-        c = wide[f, t, pl.ds(WO + SUB * j, SUB), :]
-        e = east_of(c, wide[f, t + 1, pl.ds(WO + SUB * j, SUB), :])
-        n = wide[f, t, pl.ds(WO + 1 + SUB * j, SUB), :]
-        return c, e, n
+    def near2d(buf, first, t):
+        c = buf[t, pl.ds(first, SUB), :]
+        return c, east_of(c, buf[t + 1, pl.ds(first, SUB), :]), buf[t, pl.ds(first + 1, SUB), :]
+
+    depth = wide.at[3]
 
     def momentum(lt, j):
         rc, rn, rs = pl.ds(RO + SUB * j, SUB), pl.ds(RO + 1 + SUB * j, SUB), pl.ds(RO - 1 + SUB * j, SUB)
@@ -289,10 +280,10 @@
         fu, fv = corio(row * NR + SUB * j, total_rows)
         fu4 = 0.25 * fu
         fv4 = 0.25 * fv
-        c0, ce, cn = near2d(4, lt, j)
+        c0, ce, cn = near2d(cnt, RO + SUB * j, lt)
         lu = jnp.minimum(c0, ce)
         lv = jnp.minimum(c0, cn)
-        d0, de, dn = near2d(3, lt, j)
+        d0, de, dn = near2d(depth, WO + SUB * j, lt)
         hu = 0.5 * (d0 + de)
         hv = 0.5 * (d0 + dn)
         lu_o[lt, ro, :] = lu
@@ -348,68 +339,73 @@
         abuf[0, lt, rw, :] = jnp.where(lu > ZERO, scale * hu * ((mu - su) * iu), ZERO)
         abuf[1, lt, rw, :] = jnp.where(lv > ZERO, scale * hv * ((mv - sv) * iv), ZERO)
 
-    def momentum_inner(i, _):
-        momentum(lax.rem(i, 4), 1 + i // 4)
-        return 0
-    lax.fori_loop(0, SUB, momentum_inner, 0)
-
-    @pl.when(has_s)
-    def _():
-        for cp in (to_n[0], to_n[1], to_n[2], to_n[3]):
-            cp.wait_recv()
-
-    @pl.when(has_n)
-    def _():
-        for cp in (to_s[0], to_s[1], to_s[2], to_s[3], to_s[4], to_s[5]):
-            cp.wait_recv()
+    def momentum_free(i, _):
+        momentum(1 + lax.rem(i, 2), 1 + i // 2)
+        return 0
+
+    def momentum_side(i, _):
+        momentum(3 * lax.rem(i, 2), 1 + i // 2)
+        return 0
+
+    def momentum_ends(i, _):
+        momentum(lax.rem(i, 4), 3 * (i // 4))
+        return 0
+
+    lax.fori_loop(0, 4, momentum_free, 0)
+
+    for cp in z_wide + [z_col]:
+        cp.wait_recv()
+
+    def unpack(f, _):
+        east, west = pk_r[f, 0], pk_r[f, 1]
+        for k in range(NL):
+            for j in range(4):
+                slot = 4 * k + j
+                rows = pl.ds(RO + SUB * j, SUB)
+                fb[f, 5, k, rows, :] = pltpu.roll(east, LANE - slot, 1) if slot else east
+                fb[f, 0, k, rows, :] = pltpu.roll(west, LANE - 1 - slot, 1)
+        return 0
+    lax.fori_loop(0, 4, unpack, 0)
+    for j in range(4):
+        rows = pl.ds(WO + SUB * j, SUB)
+        wide[3, 4, rows, :] = pltpu.roll(wide[1, 4, rows, :], LANE // 2, 1)
+
+    def pressure_east(i, _):
+        pressure(5, pl.multiple_of(RO + SUB * i, SUB))
+        return 0
+    lax.fori_loop(0, 4, pressure_east, 0)
+    lax.fori_loop(0, 4, momentum_side, 0)
+
+    arrived(n_first + n_vel, s_first + s_vel + s_tra)
 
     def pressure_north(i, _):
         pressure(1 + i, RO + NR)
         return 0
     lax.fori_loop(0, 4, pressure_north, 0)
-
-    def momentum_outer(i, _):
-        momentum(lax.rem(i, 4), 3 * (i // 4))
-        return 0
-    lax.fori_loop(0, SUB, momentum_outer, 0)
-
-    for f in range(2):
-        for j in range(4):
-            rows = pl.ds(WO + SUB * j, SUB)
-            asend[f, pl.ds(SUB * j, SUB), :] = jnp.where(half, abuf[f, 0, rows, :], abuf[f, 3, rows, :])
-
-    def arows(b):
-        return abuf.at[:, own4, pl.ds(WO, NR), :], abuf.at[:, own4, pl.ds(b, NR), :]
-
-    force_z = remote(20, asend, abuf.at[:, 4, pl.ds(WO, NR), :], dev(0, ocol))
-    force_n = [remote(21, *arows(WO - NR), dev(1, col)), remote(23, asend, abuf.at[:, 4, pl.ds(WO - NR, NR), :], dev(1, ocol))]
-    force_s = [remote(22, *arows(WO + NR), dev(-1, col)), remote(24, asend, abuf.at[:, 4, pl.ds(WO + NR, NR), :], dev(-1, ocol))]
-    force_z.start()
-
-    @pl.when(has_n)
-    def _():
-        for cp in force_n:
-            cp.start()
-
-    @pl.when(has_s)
-    def _():
-        for cp in force_s:
-            cp.start()
-
-    @pl.when(has_s)
-    def _():
-        for cp in (to_n[4], to_n[5]):
-            cp.wait_recv()
+    lax.fori_loop(0, SUB, momentum_ends, 0)
+
+    for j in range(4):
+        asend[pl.ds(SUB * j, SUB), :] = paired(abuf, 0, 1, WO + SUB * j)
+
+    def force_corner(a, b, d):
+        return remote(asend.at[pl.ds(a - WO, NH), :], abuf.at[0, 4, pl.ds(b, NH), :], dev(d, ocol))
+
+    z_force = remote(asend, abuf.at[0, 4, pl.ds(WO, NR), :], dev(0, ocol))
+    n_force = [rows2(abuf, 0, 2, n_src, n_dst, 1), force_corner(n_src, n_dst, 1)]
+    s_force = [rows2(abuf, 0, 2, s_src, s_dst, -1), force_corner(s_src, s_dst, -1)]
+    z_force.start()
+    both(s_force, n_force, lambda cp: cp.start())
+
+    arrived(n_tra, [])
 
     def tracers(lt, j):
         rc, rn, rs = pl.ds(RO + SUB * j, SUB), pl.ds(RO + 1 + SUB * j, SUB), pl.ds(RO - 1 + SUB * j, SUB)
         ro = pl.ds(SUB * j, SUB)
         t = lt + 1
-        rw = pl.ds(WO + SUB * j, SUB)
-        c0 = wide[4, lt, rw, :]
+        c0 = cnt[lt, rc, :]
         left = lax.rem(lt + 4, 5)
-        luw = jnp.minimum(c0, west_of(c0, wide[4, left, rw, :]))
-        lvs = jnp.minimum(c0, wide[4, lt, pl.ds(WO - 1 + SUB * j, SUB), :])
+        luw = jnp.minimum(c0, west_of(c0, cnt[left, rc, :]))
+        lvs = jnp.minimum(c0, cnt[lt, rs, :])
         lu = lu_o[lt, ro, :]
         lv = lv_o[lt, ro, :]
         half_dt = 0.5 * TIME_STEP
@@ -448,40 +444,12 @@
         return 0
     lax.fori_loop(0, 16, tracers_all, 0)
 
-    @pl.when(has_s)
-    def _():
-        for cp in (to_n[6], to_n[7], to_n[SUB]):
-            cp.wait_recv()
-
-    @pl.when(has_n)
-    def _():
-        for cp in (to_s[6], to_s[7], to_s[SUB]):
-            cp.wait_recv()
-
-    force_z.wait_recv()
-
-    @pl.when(has_s)
-    def _():
-        for cp in force_n:
-            cp.wait_recv()
-
-    @pl.when(has_n)
-    def _():
-        for cp in force_s:
-            cp.wait_recv()
-
-    for cp in east_w + [force_z]:
+    z_force.wait_recv()
+    arrived(n_far + n_force, s_far + s_force)
+
+    for cp in z_wide + [z_col, z_force]:
         cp.wait_send()
-
-    @pl.when(has_n)
-    def _():
-        for cp in to_n + force_n:
-            cp.wait_send()
-
-    @pl.when(has_s)
-    def _():
-        for cp in to_s + force_s:
-            cp.wait_send()
+    both(s_first + s_vel + s_tra + s_far + s_force, n_first + n_vel + n_tra + n_far + n_force, lambda cp: cp.wait_send())
 
 
 def finish_kernel(n_row, n_sub, w_ref,
@@ -507,40 +475,35 @@
         base = SUB + SUB * i
         rows = pl.ds(base, SUB)
         rown = pl.ds(base + 1, SUB)
-        fu, fv = corio(row * NR + SUB * i - NR, total_rows)
+        first = row * NR + SUB * i - NR
+        fu, fv = corio(first, total_rows)
+        place = first + lax.broadcasted_iota(jnp.int32, (SUB, LANE), 0)
+        inside = place >= 0
+        wet_u = jnp.logical_and(inside, place < n_row * NR).astype(F32)
+        wet_v = jnp.logical_and(inside, place < n_row * NR - 1).astype(F32)
         for t in range(5):
             right = (t + 1) % 5
-            c0 = wide[4, t, rows, :]
-            wet_u = (jnp.minimum(c0, east_of(c0, wide[4, right, rows, :])) > ZERO).astype(F32)
-            wet_v = (jnp.minimum(c0, wide[4, t, rown, :]) > ZERO).astype(F32)
             d0 = wide[3, t, rows, :]
-            scale = dtb * dtb * GRAVITY * 0.5
+            scale = 0.5 * dtb * dtb * GRAVITY
             bu[t, rows, :] = wet_u * (scale * (d0 + east_of(d0, wide[3, right, rows, :])))
             bv[t, rows, :] = wet_v * (scale * (d0 + wide[3, t, rown, :]))
             cfu[t, rows, :] = wet_u * ((0.25 * dtb) * fu)
             cfv[t, rows, :] = wet_v * ((0.25 * dtb) * fv)
             mku[t, rows, :] = wet_u
             mkv[t, rows, :] = wet_v
-            tu[0, t, rows, :] = dtb * wide[1, t, rows, :]
-            tv[0, t, rows, :] = dtb * wide[2, t, rows, :]
-        return 0
+            tu[0, t, rows, :] = dtb * wide[2, t, rows, :]
+            tv[0, t, rows, :] = dtb * wide[1, t, rows, :]
+        return 0
+
+    for i in range(12):
+        rows = pl.ds(SUB + SUB * i, SUB)
+        for f in range(2):
+            wide[f + 2, 4, rows, :] = pltpu.roll(wide[f, 4, rows, :], LANE // 2, 1)
+        abuf[1, 4, rows, :] = pltpu.roll(abuf[0, 4, rows, :], LANE // 2, 1)
     lax.fori_loop(0, 12, setup, 0)
-    for t in range(5):
-        for a in (0, 1):
-            for start in (0, 104):
-                tu[a, t, pl.ds(start, SUB), :] = zero8
-                tv[a, t, pl.ds(start, SUB), :] = zero8
-        for i in range(2):
-            xs[t, pl.ds(104 * i, SUB), :] = zero8
-    for i in range(13):
-        for t in range(5):
-            tu[1, t, pl.ds(SUB * i + SUB, SUB), :] = zero8
-            tv[1, t, pl.ds(SUB * i + SUB, SUB), :] = zero8
-            xs[t, pl.ds(SUB * i + SUB, SUB), :] = zero8
     for t in range(NT):
-        for j in range(4):
-            acu[t, pl.ds(SUB * j, SUB), :] = zero8
-            acv[t, pl.ds(SUB * j, SUB), :] = zero8
+        acu[t] = jnp.zeros((NR, LANE), F32)
+        acv[t] = jnp.zeros((NR, LANE), F32)
 
     def subcycle(n, cur, lo, hi, first=False):
         nxt = 1 - cur
@@ -632,9 +595,8 @@
         smem = pl.BlockSpec(memory_space=pltpu.SMEM)
         cube_v = pltpu.VMEM((NT, NL, NR, LANE), F32)
         flat_v = pltpu.VMEM((NT, NR, LANE), F32)
-        pad3 = pltpu.VMEM((6, NL, 48, LANE), F32)
         wide1 = pltpu.VMEM((5, WR, LANE), F32)
-        wide_v = pltpu.VMEM((5, 5, WR, LANE), F32)
+        wide_v = pltpu.VMEM((4, 5, WR, LANE), F32)
         force_v = pltpu.VMEM((2, 5, WR, LANE), F32)
         sems = pltpu.SemaphoreType.DMA
         outs = [cube_v] * 4 + [wide_v, force_v] + [flat_v] * 6
@@ -643,12 +605,15 @@
             out_shape=outs,
             in_specs=[hbm] * 9,
             out_specs=[vmem] * len(outs),
-            scratch_shapes=[pad3] * 5 + [
-                pltpu.VMEM((5, NR, LANE), F32),
+            scratch_shapes=[
+                pltpu.VMEM((4, 6, NL, RO + NR + SUB, LANE), F32),
+                pltpu.VMEM((6, NL, RO + NR + SUB, LANE), F32),
+                pltpu.VMEM((5, RO + NR + SUB, LANE), F32),
+                pltpu.VMEM((3, NR, LANE), F32),
                 pltpu.VMEM((NT, NR, LANE), jnp.int32),
-                pltpu.VMEM((SUB, SUB, LANE), F32),
-                pltpu.VMEM((SUB, SUB, LANE), F32),
-                pltpu.VMEM((2, NR, LANE), F32),
+                pltpu.VMEM((4, 2, SUB, LANE), F32),
+                pltpu.VMEM((4, 2, SUB, LANE), F32),
+                pltpu.VMEM((NR, LANE), F32),
                 sems((16,)), sems((20,)), sems((N_COPY,)), sems((N_COPY,)),
             ],
             compiler_params=pltpu.CompilerParams(collective_id=0, has_side_effects=True, vmem_limit_bytes=VMEM_MAIN),

time: 44 us -> 36.2 us (0.82)
  Pallas kernels: 43.2 us -> 35.5 us
    pallas_call x1, Pallas kernels: 31.1 us -> 24 us  [step(): pl.pallas_call(functools.partial(ocean_kernel, n_row, n_sub), out_shape=o...]
    pallas_call x1, Pallas kernels: 12.1 us -> 11.5 us  [step(): pl.pallas_call(functools.partial(finish_kernel, n_row, n_sub), out_shape=...]
where the time goes in v2:
time: 36.2 us; the launch traced here: 36.1 us
  Pallas kernels  35.5 us (98%)
  between operations  0.66 us (2%)
    pallas_call x1, Pallas kernels, step(): pl.pallas_call(functools.partial(ocean_kernel, n_row, n_sub), out_shape=o...  24 us
    pallas_call x1, Pallas kernels, step(): pl.pallas_call(functools.partial(finish_kernel, n_row, n_sub), out_shape=...  11.5 us

profile of v2, /device:TPU:0, one launch (start us, length us, event | category | flops | bytes accessed | tf_op | source)
XLA Modules:
  0.0 36.1 jit_solution(16858857461495041843)
XLA Ops:
  0.6 0.0 copy-start
  0.6 24.0 %ocean.1 = (f32[4,31,32,128]{3,2,1,0:T(8,128)S(1)}, f32[4,31,32,128]{3,2,1,0:T(8,128)S(1)}, f32[4,31,32,128]{3,2,1,0:T(8,128)S(1)}, f32[4,31,32,128]{3,2,1,0:T(8...) custom-call(f32[31,32,512]{2,1,0:T(8,128)} %u_in.1, ...), custom_call_target="tpu_custom_call" | custom-call | tf_op jit(solution)/shard_map/ocean/pallas_call | solution.py:603
  24.6 0.0 copy-done
  24.6 11.5 %finish.1 = (f32[32,512]{1,0:T(8,128)}, f32[32,512]{1,0:T(8,128)}, f32[32,512]{1,0:T(8,128)}, f32[31,32,512]{2,1,0:T(8,128)}, f32[31,32,512]{2,1,0:T(8,128)}, /*...) custom-call(f32[30]{0:T(128)S(1)} %copy-done, f32[4,31,32,128]{3,2,1,0:T(8,128)S(1)} %get-tuple-element.19.us, ...), custom_call_target="tpu_custom_call" | custom-call | tf_op jit(solution)/shard_map/finish/pallas_call | solution.py:624
Async XLA Ops:
  0.6 24.0 %copy-start = (f32[30]{0:T(128)S(1)}, f32[30]{0:T(128)}, u32[]{:S(2)}) copy-start(f32[30]{0:T(128)} %w_ref.1) | copy-start | bytes 364

commit v3 on v2

--- a/solution.py
+++ b/solution.py
@@ -30,7 +30,7 @@
 RO = 8
 WO = 40
 WR = 112
-N_COPY = 32
+N_COPY = 40
 NH = 30
 VMEM_MAIN = 40 * 1024 * 1024
 VMEM_FINISH = 12 * 1024 * 1024
@@ -55,12 +55,17 @@
     return lax.broadcasted_iota(jnp.int32, (SUB, LANE), 1)
 
 
-def west_of(own, left):
-    return pltpu.roll(jnp.where(lanes() == 127, left, own), 1, 1)
-
-
-def east_of(own, right):
-    return pltpu.roll(jnp.where(lanes() == 0, right, own), 127, 1)
+def movers(height=SUB):
+    here = lax.broadcasted_iota(jnp.int32, (height, LANE), 1)
+    first, last = here == 0, here == LANE - 1
+
+    def west_of(own, left):
+        return pltpu.roll(lax.select(last, left, own), 1, 1)
+
+    def east_of(own, right):
+        return pltpu.roll(lax.select(first, right, own), LANE - 1, 1)
+
+    return west_of, east_of
 
 
 def corio(first, total_rows):
@@ -73,7 +78,7 @@
 def ocean_kernel(n_row, n_sub,
                  u_in, v_in, t_in, s_in, eta_in, tu_in, tv_in, dep_in, cnt_in,
                  us_o, vs_o, tn_o, sn_o, wide, abuf, lu_o, lv_o, hu_s, hv_s, mu_s, mv_s,
-                 fb, pb, cnt, wsend, cnt_i, pk_s, pk_r, asend,
+                 fb, pb, uw_b, ve_b, near, relay, wsend, cnt_i, pk_s, pk_r, asend,
                  in_sem, w_sem, send, recv):
     row = lax.axis_index('row')
     col = lax.axis_index('col')
@@ -85,6 +90,13 @@
     used = []
     ub, vb, tb, sb = (fb.at[f] for f in range(4))
     zero8 = jnp.zeros((SUB, LANE), F32)
+    west_of, east_of = movers()
+    west_all, east_all = movers(NR)
+    all_rows = pl.ds(RO, NR)
+    cnt, depth = near.at[0], near.at[1]
+    half_row = n_row // 2
+    up, down = row == half_row - 1, row == half_row
+    first_row, last_row = row == 0, row == n_row - 1
 
     def dev(step, c):
         return {'row': row + step, 'col': c}
@@ -119,9 +131,11 @@
             wloads[f, t] = pltpu.make_async_copy(src.at[:, pl.ds(LANE * t, LANE)], dst, w_sem.at[f * NT + t])
     for f, src in enumerate((u_in, v_in, t_in, s_in)):
         for t in range(NT):
-            loads[f, t] = pltpu.make_async_copy(src.at[:, :, pl.ds(LANE * t, LANE)], fb.at[f, t + 1, :, pl.ds(RO, NR), :], in_sem.at[f * NT + t])
+            loads[f, t] = pltpu.make_async_copy(src.at[:, :, pl.ds(LANE * t, LANE)], fb.at[f, t, :, pl.ds(RO, NR), :], in_sem.at[f * NT + t])
+    for t in range(NT):
+        wloads[5, t] = pltpu.make_async_copy(dep_in.at[:, pl.ds(LANE * t, LANE)], near.at[1, t, pl.ds(RO, NR), :], w_sem.at[5 * NT + t])
     start(wloads.values())
-    order = [(f, t) for f in range(4) for t in (0, 3)] + [(f, t) for f in (0, 1, 2, 3) for t in (1, 2)]
+    order = [(f, t) for g in (0, 2) for tiles in ((0, 3), (1, 2)) for f in (g, g + 1) for t in tiles]
     start([loads[key] for key in order])
 
     for i in range(5):
@@ -144,18 +158,28 @@
         for c in (col, ocol):
             pl.semaphore_signal(barrier, inc=1, device_id=dev(-1, c), device_id_type=MESH)
 
+    def greet(rows_of):
+        for d in rows_of:
+            pl.semaphore_signal(barrier, inc=1, device_id=dev(d, col), device_id_type=MESH)
+
+    pl.when(up)(lambda: greet((half_row, 1 - half_row)))
+    pl.when(down)(lambda: greet((half_row - 1, -half_row)))
+    pl.when(first_row)(lambda: greet((half_row - 1, half_row)))
+    pl.when(last_row)(lambda: greet((-half_row, 1 - half_row)))
+
     def fill(first3, first2):
         def body(i, _):
             for f in range(4):
                 fb[f, i, :, pl.ds(first3, SUB), :] = jnp.zeros((NL, SUB, LANE), F32)
             return 0
-        lax.fori_loop(0, 6, body, 0)
+        lax.fori_loop(0, 5, body, 0)
         for i in range(5):
             for f in range(4):
                 wide[f, i, pl.ds(first2, NR), :] = jnp.zeros((NR, LANE), F32)
             for f in range(2):
                 abuf[f, i, pl.ds(first2, NR), :] = jnp.zeros((NR, LANE), F32)
-            cnt[i, pl.ds(first3, SUB), :] = zero8
+            for f in range(2):
+                near[f, i, pl.ds(first3, SUB), :] = zero8
 
     @pl.when(jnp.logical_not(has_s))
     def _():
@@ -186,104 +210,159 @@
         for f in range(2):
             wsend[f, mine, :] = paired(wide, f, f + 2, first)
         own = pl.ds(RO + SUB * j, SUB)
-        wsend[2, mine, :] = jnp.where(outer, cnt[0, own, :], cnt[3, own, :])
-
-    barrier_count = 1 + 2 * has_n.astype(jnp.int32) + 2 * has_s.astype(jnp.int32)
+        for f in range(2):
+            wsend[2 + f, mine, :] = jnp.where(outer, near[f, 0, own, :], near[f, 3, own, :])
+
+    round_about = jnp.logical_or(jnp.logical_or(up, down), jnp.logical_or(first_row, last_row))
+    barrier_count = 1 + 2 * has_n.astype(jnp.int32) + 2 * has_s.astype(jnp.int32) + 2 * round_about.astype(jnp.int32)
     pl.semaphore_wait(barrier, barrier_count)
 
     own4 = pl.ds(0, NT)
-    mid4 = pl.ds(1, NT)
     two = pl.ds(0, 2)
     top, low, north, south = RO + NR - 1, RO, RO + NR, RO - 1
     n_src, n_dst, s_src, s_dst = WO + NR - NH, WO - NH, WO, WO + NR
 
     def rows3(f, a, b, d):
-        return remote(fb.at[f, mid4, :, pl.ds(a, 1), :], fb.at[f, mid4, :, pl.ds(b, 1), :], dev(d, col))
+        return remote(fb.at[f, own4, :, pl.ds(a, 1), :], fb.at[f, own4, :, pl.ds(b, 1), :], dev(d, col))
 
     def rows2(buf, f, nf, a, b, d):
         return remote(buf.at[pl.ds(f, nf), own4, pl.ds(a, NH), :], buf.at[pl.ds(f, nf), own4, pl.ds(b, NH), :], dev(d, col))
 
     def row1(a, b, d):
-        return remote(cnt.at[own4, pl.ds(a, 1), :], cnt.at[own4, pl.ds(b, 1), :], dev(d, col))
+        return remote(near.at[:, own4, pl.ds(a, 1), :], near.at[:, own4, pl.ds(b, 1), :], dev(d, col))
 
     def corner(a, b, d):
         return remote(wsend.at[two, pl.ds(a - WO, NH), :], wide.at[two, 4, pl.ds(b, NH), :], dev(d, ocol))
 
     z_wide = [
-        remote(wsend.at[2], cnt.at[4, pl.ds(RO, NR), :], dev(0, ocol)),
+        remote(wsend.at[pl.ds(2, 2)], near.at[:, 4, pl.ds(RO, NR), :], dev(0, ocol)),
         remote(wsend.at[two], wide.at[two, 4, pl.ds(WO, NR), :], dev(0, ocol)),
     ]
-    n_first = [row1(top, south, 1), rows2(wide, 3, 1, n_src, n_dst, 1)]
-    s_first = [row1(low, north, -1), rows2(wide, 3, 1, s_src, s_dst, -1)]
+    n_first = [row1(top, south, 1)]
+    s_first = [row1(low, north, -1)]
+
+    def via(src_row, dst_row, there, onward):
+        leg1 = remote(wide.at[:, own4, pl.ds(src_row, NH), :], relay, dev(there, col))
+        leg2 = remote(relay, wide.at[:, own4, pl.ds(dst_row, NH), :], dev(onward, col))
+        return leg1, leg2
+
+    n_leg1, n_leg2 = via(n_src, n_dst, half_row, 1 - half_row)
+    s_leg1, s_leg2 = via(s_src, s_dst, -half_row, half_row - 1)
+    pl.when(up)(n_leg1.start)
+    pl.when(down)(s_leg1.start)
     start(z_wide)
     both(s_first, n_first, lambda cp: cp.start())
 
-    for f in (0, 1):
-        for t in (0, 3, 1, 2):
+    def slot(k, j):
+        return (4 * k + j) // 64, 2 * ((4 * k + j) % 64)
+
+    def pack(half_of, _):
+        here = lanes()
+        first = lax.broadcasted_iota(jnp.int32, (NR, LANE), 1) == 0
+        acc = {}
+        for k in range(NL):
+            for f in range(2):
+                field = 2 * half_of + f
+                both_edges = lax.select(first, fb[field, 0, k, all_rows, :], fb[field, 3, k, all_rows, :])
+                for j in range(4):
+                    word, at = slot(k, j)
+                    pair = both_edges[SUB * j:SUB * (j + 1)]
+                    if at:
+                        mine = jnp.logical_or(here == at, here == at - 1)
+                        acc[f, word] = lax.select(mine, pltpu.roll(pair, at, 1), acc[f, word])
+                    else:
+                        acc[f, word] = pair
+        for f, word in acc:
+            pk_s[2 * half_of + f, word] = acc[f, word]
+        return 0
+
+    def unpack(half_of, _):
+        for f in range(2):
+            field = 2 * half_of + f
+            got = [pk_r[field, word] for word in range(2)]
+            for k in range(NL):
+                parts = []
+                for j in range(4):
+                    word, at = slot(k, j)
+                    parts.append(pltpu.roll(got[word], LANE - at, 1) if at else got[word])
+                fb[field, 4, k, all_rows, :] = jnp.concatenate(parts, axis=0)
+        return 0
+
+    def shift_u(t):
+        for k in range(NL):
+            uw_b[t, k, all_rows, :] = west_all(ub[t, k, all_rows, :], ub[lax.rem(t + 4, 5), k, all_rows, :])
+
+    def shift_v(t):
+        for k in range(NL):
+            ve_b[t, k, all_rows, :] = east_all(vb[t, k, all_rows, :], vb[t + 1, k, all_rows, :])
+
+    for t in (0, 3, 1, 2):
+        for f in (0, 1):
             loads[f, t].wait()
     n_vel = [rows3(0, top, south, 1), rows3(1, top, south, 1),
-             remote(fb.at[1, 1, :, pl.ds(top, 1), :], fb.at[1, 5, :, pl.ds(south, 1), :], dev(1, ocol))]
+             remote(fb.at[1, 0, :, pl.ds(top, 1), :], fb.at[1, 4, :, pl.ds(south, 1), :], dev(1, ocol))]
     s_vel = [rows3(0, low, north, -1), rows3(1, low, north, -1),
-             remote(fb.at[0, 4, :, pl.ds(low, 1), :], fb.at[0, 0, :, pl.ds(north, 1), :], dev(-1, ocol))]
+             remote(fb.at[0, 3, :, pl.ds(low, 1), :], fb.at[0, 4, :, pl.ds(north, 1), :], dev(-1, ocol))]
     both(s_vel, n_vel, lambda cp: cp.start())
-    for f in (2, 3):
-        for t in (0, 3, 1, 2):
+
+    def shift_own(t, _):
+        shift_u(t + 1)
+        shift_v(t)
+        return 0
+    lax.fori_loop(0, 3, shift_own, 0)
+
+    for t in (0, 3, 1, 2):
+        for f in (2, 3):
             loads[f, t].wait()
     n_tra = [rows3(2, top, south, 1), rows3(3, top, south, 1)]
     s_tra = [rows3(2, low, north, -1), rows3(3, low, north, -1)]
-    n_far = [rows2(wide, 0, 3, n_src, n_dst, 1), corner(n_src, n_dst, 1)]
-    s_far = [rows2(wide, 0, 3, s_src, s_dst, -1), corner(s_src, s_dst, -1)]
-    both(s_tra + s_far, n_tra + n_far, lambda cp: cp.start())
-
-    def pack(f, _):
-        here = lanes()
-        east, west = zero8, zero8
-        for k in range(NL):
-            for j in range(4):
-                slot = 4 * k + j
-                rows = pl.ds(RO + SUB * j, SUB)
-                east = jnp.where(here == slot, pltpu.roll(fb[f, 1, k, rows, :], slot, 1) if slot else fb[f, 1, k, rows, :], east)
-                west = jnp.where(here == slot, pltpu.roll(fb[f, 4, k, rows, :], slot + 1, 1), west)
-        pk_s[f, 0] = east
-        pk_s[f, 1] = west
-        return 0
-    lax.fori_loop(0, 4, pack, 0)
+    n_far, s_far = rows2(wide, 0, 4, n_src, n_dst, 1), rows2(wide, 0, 4, s_src, s_dst, -1)
+    n_cor, s_cor = corner(n_src, n_dst, 1), corner(s_src, s_dst, -1)
+    both(s_tra, n_tra, lambda cp: cp.start())
+    far_n, far_s = jnp.logical_and(has_n, jnp.logical_not(up)), jnp.logical_and(has_s, jnp.logical_not(down))
+    pl.when(far_n)(n_far.start)
+    pl.when(far_s)(s_far.start)
+    both([s_cor], [n_cor], lambda cp: cp.start())
+    lax.fori_loop(0, 2, pack, 0)
     z_col = remote(pk_s, pk_r, dev(0, ocol))
     z_col.start()
 
     p_unit = 0.5 * BC_GRAVITY / NL
 
-    def pressure(t, start):
-        rows = pl.ds(start, SUB)
-        total = zero8
+    def pressure(t, rows, height):
+        total = jnp.zeros((height, LANE), F32)
         for k in range(NL):
             part = (p_unit * CONTRACT_S) * sb[t, k, rows, :] - (p_unit * EXPAND_T) * tb[t, k, rows, :]
             here = total + part
             pb[t, k, rows, :] = here
             total = here + part
 
-    def pressure_own(i, _):
-        pressure(1 + i // 4, pl.multiple_of(RO + SUB * lax.rem(i, 4), SUB))
-        return 0
-    lax.fori_loop(0, 16, pressure_own, 0)
+    def pressure_own(t, _):
+        pressure(t, all_rows, NR)
+        return 0
+    lax.fori_loop(0, NT, pressure_own, 0)
 
     def near2d(buf, first, t):
         c = buf[t, pl.ds(first, SUB), :]
         return c, east_of(c, buf[t + 1, pl.ds(first, SUB), :]), buf[t, pl.ds(first + 1, SUB), :]
 
-    depth = wide.at[3]
-
-    def momentum(lt, j):
+    def pick(mask, inner, last):
+        return lax.select(mask, jnp.full((SUB, LANE), inner, F32), jnp.full((SUB, LANE), last, F32))
+
+    def keep(mask, value):
+        return lax.select(mask, value, zero8)
+
+    def momentum(lt, j, at_south=False, at_north=False):
         rc, rn, rs = pl.ds(RO + SUB * j, SUB), pl.ds(RO + 1 + SUB * j, SUB), pl.ds(RO - 1 + SUB * j, SUB)
         ro = pl.ds(SUB * j, SUB)
-        t = lt + 1
+        t, right, left = lt, lax.rem(lt + 1, 5), lax.rem(lt + 4, 5)
         fu, fv = corio(row * NR + SUB * j, total_rows)
         fu4 = 0.25 * fu
         fv4 = 0.25 * fv
         c0, ce, cn = near2d(cnt, RO + SUB * j, lt)
         lu = jnp.minimum(c0, ce)
         lv = jnp.minimum(c0, cn)
-        d0, de, dn = near2d(depth, WO + SUB * j, lt)
+        d0, de, dn = near2d(depth, RO + SUB * j, lt)
         hu = 0.5 * (d0 + de)
         hv = 0.5 * (d0 + dn)
         lu_o[lt, ro, :] = lu
@@ -295,41 +374,40 @@
         for k in range(NL):
             u = ub[t, k, rc, :]
             v = vb[t, k, rc, :]
-            uw = west_of(u, ub[t - 1, k, rc, :])
-            ue = east_of(u, ub[t + 1, k, rc, :])
+            uw = uw_b[t, k, rc, :]
+            ue = east_of(u, ub[right, k, rc, :])
             un = ub[t, k, rn, :]
             us = ub[t, k, rs, :]
-            unw = west_of(un, ub[t - 1, k, rn, :])
-            vw = west_of(v, vb[t - 1, k, rc, :])
-            vright = vb[t + 1, k, rc, :]
-            ve = east_of(v, vright)
+            unw = west_of(un, ub[left, k, rn, :]) if at_north else uw_b[t, k, rn, :]
+            vw = west_of(v, vb[left, k, rc, :])
+            ve = ve_b[t, k, rc, :]
             vn = vb[t, k, rn, :]
             vs = vb[t, k, rs, :]
-            v2 = v + vs
-            v4 = v2 + east_of(v2, vright + vb[t + 1, k, rs, :])
+            vse = east_of(vs, vb[right, k, rs, :]) if at_south else ve_b[t, k, rs, :]
+            v4 = (v + ve) + (vs + vse)
             u4 = (u + uw) + (un + unw)
             p = pb[t, k, rc, :]
-            pe = east_of(p, pb[t + 1, k, rc, :])
+            pe = east_of(p, pb[right, k, rc, :])
             pn = pb[t, k, rn, :]
             ustar = u + (v4 * (fu4 - 0.125 * (un - us)) - 0.5 * u * (ue - uw) - (pe - p))
             vstar = v - (u4 * (fv4 + 0.125 * (ve - vw)) + 0.5 * v * (vn - vs) + (pn - p))
-            yu = (ustar + yu) * (jnp.where(lu > k + 1, VISC_IN[k], VISC_END[k]) if k < NL - 1 else VISC_END[k])
-            yv = (vstar + yv) * (jnp.where(lv > k + 1, VISC_IN[k], VISC_END[k]) if k < NL - 1 else VISC_END[k])
+            yu = (ustar + yu) * (pick(lu > k + 1, VISC_IN[k], VISC_END[k]) if k < NL - 1 else VISC_END[k])
+            yv = (vstar + yv) * (pick(lv > k + 1, VISC_IN[k], VISC_END[k]) if k < NL - 1 else VISC_END[k])
             us_o[lt, k, ro, :] = yu
             vs_o[lt, k, ro, :] = yv
-            su = su + jnp.where(lu > k, u, ZERO)
-            sv = sv + jnp.where(lv > k, v, ZERO)
+            su = su + keep(lu > k, u)
+            sv = sv + keep(lv > k, v)
         mu, mv = zero8, zero8
         xu, xv = zero8, zero8
         for k in reversed(range(NL)):
-            xu = us_o[lt, k, ro, :] + (jnp.where(lu > k + 1, VISC_IN[k] * xu, ZERO) if k < NL - 1 else ZERO)
-            xv = vs_o[lt, k, ro, :] + (jnp.where(lv > k + 1, VISC_IN[k] * xv, ZERO) if k < NL - 1 else ZERO)
+            xu = us_o[lt, k, ro, :] + (keep(lu > k + 1, VISC_IN[k] * xu) if k < NL - 1 else ZERO)
+            xv = vs_o[lt, k, ro, :] + (keep(lv > k + 1, VISC_IN[k] * xv) if k < NL - 1 else ZERO)
             outu = (ONE / VISC_R) * xu
             outv = (ONE / VISC_R) * xv
             us_o[lt, k, ro, :] = outu
             vs_o[lt, k, ro, :] = outv
-            mu = mu + jnp.where(lu > k, outu, ZERO)
-            mv = mv + jnp.where(lv > k, outv, ZERO)
+            mu = mu + keep(lu > k, outu)
+            mv = mv + keep(lv > k, outv)
         iu = ONE / jnp.maximum(lu, ONE)
         iv = ONE / jnp.maximum(lv, ONE)
         mu_s[lt, ro, :] = mu * iu
@@ -339,71 +417,87 @@
         abuf[0, lt, rw, :] = jnp.where(lu > ZERO, scale * hu * ((mu - su) * iu), ZERO)
         abuf[1, lt, rw, :] = jnp.where(lv > ZERO, scale * hv * ((mv - sv) * iv), ZERO)
 
-    def momentum_free(i, _):
-        momentum(1 + lax.rem(i, 2), 1 + i // 2)
-        return 0
-
-    def momentum_side(i, _):
-        momentum(3 * lax.rem(i, 2), 1 + i // 2)
-        return 0
-
-    def momentum_ends(i, _):
-        momentum(lax.rem(i, 4), 3 * (i // 4))
-        return 0
-
-    lax.fori_loop(0, 4, momentum_free, 0)
-
-    for cp in z_wide + [z_col]:
-        cp.wait_recv()
-
-    def unpack(f, _):
-        east, west = pk_r[f, 0], pk_r[f, 1]
-        for k in range(NL):
-            for j in range(4):
-                slot = 4 * k + j
-                rows = pl.ds(RO + SUB * j, SUB)
-                fb[f, 5, k, rows, :] = pltpu.roll(east, LANE - slot, 1) if slot else east
-                fb[f, 0, k, rows, :] = pltpu.roll(west, LANE - 1 - slot, 1)
-        return 0
-    lax.fori_loop(0, 4, unpack, 0)
-    for j in range(4):
-        rows = pl.ds(WO + SUB * j, SUB)
-        wide[3, 4, rows, :] = pltpu.roll(wide[1, 4, rows, :], LANE // 2, 1)
-
-    def pressure_east(i, _):
-        pressure(5, pl.multiple_of(RO + SUB * i, SUB))
-        return 0
-    lax.fori_loop(0, 4, pressure_east, 0)
-    lax.fori_loop(0, 4, momentum_side, 0)
+    def middle_rows(i, _):
+        odd, later = lax.rem(i, 2), i // 4
+
+        @pl.when(jnp.logical_and(i == 6, last_row))
+        def _():
+            n_leg1.wait_recv()
+            n_leg2.start()
+
+        @pl.when(jnp.logical_and(i == 6, first_row))
+        def _():
+            s_leg1.wait_recv()
+            s_leg2.start()
+
+        @pl.when(i == 4)
+        def _():
+            for cp in (z_wide[0], z_col):
+                cp.wait_recv()
+            lax.fori_loop(0, 2, unpack, 0)
+            shift_u(0)
+            shift_v(3)
+            pressure(4, all_rows, NR)
+
+        momentum(1 + odd + later * (2 * odd - 1), 1 + lax.rem(i, 4) // 2)
+        return 0
+
+    lax.fori_loop(0, SUB, middle_rows, 0)
 
     arrived(n_first + n_vel, s_first + s_vel + s_tra)
 
     def pressure_north(i, _):
-        pressure(1 + i, RO + NR)
-        return 0
-    lax.fori_loop(0, 4, pressure_north, 0)
-    lax.fori_loop(0, SUB, momentum_ends, 0)
-
-    for j in range(4):
-        asend[pl.ds(SUB * j, SUB), :] = paired(abuf, 0, 1, WO + SUB * j)
+        for odd in range(2):
+            pressure(2 * i + odd, pl.ds(RO + NR, SUB), SUB)
+        return 0
+    lax.fori_loop(0, 2, pressure_north, 0)
 
     def force_corner(a, b, d):
         return remote(asend.at[pl.ds(a - WO, NH), :], abuf.at[0, 4, pl.ds(b, NH), :], dev(d, ocol))
 
+    def force_rows(t, a, b, d):
+        return remote(abuf.at[:, t, pl.ds(a, NH), :], abuf.at[:, t, pl.ds(b, NH), :], dev(d, col))
+
+    def force_pair(t):
+        return force_rows(t, n_src, n_dst, 1), force_rows(t, s_src, s_dst, -1)
+
     z_force = remote(asend, abuf.at[0, 4, pl.ds(WO, NR), :], dev(0, ocol))
-    n_force = [rows2(abuf, 0, 2, n_src, n_dst, 1), force_corner(n_src, n_dst, 1)]
-    s_force = [rows2(abuf, 0, 2, s_src, s_dst, -1), force_corner(s_src, s_dst, -1)]
-    z_force.start()
-    both(s_force, n_force, lambda cp: cp.start())
+    n_fcor, s_fcor = force_corner(n_src, n_dst, 1), force_corner(s_src, s_dst, -1)
+
+    force = [force_pair(t) for t in range(NT)]
+    n_force = [p[0] for p in force] + [n_fcor]
+    s_force = [p[1] for p in force] + [s_fcor]
+
+    def send_force(which):
+        both([s_force[i] for i in which], [n_force[i] for i in which], lambda cp: cp.start())
+
+    def ends(i, _):
+        t = lax.rem(3 * i, 4)
+        momentum(t, 0, at_south=True)
+        momentum(t, 3, at_north=True)
+
+        @pl.when(i == 1)
+        def _():
+            for j in range(4):
+                asend[pl.ds(SUB * j, SUB), :] = paired(abuf, 0, 1, WO + SUB * j)
+            z_force.start()
+            send_force((0, 3, 4))
+
+        @pl.when(i == 2)
+        def _():
+            send_force((2,))
+        return 0
+
+    lax.fori_loop(0, NT, ends, 0)
+    send_force((1,))
 
     arrived(n_tra, [])
 
     def tracers(lt, j):
         rc, rn, rs = pl.ds(RO + SUB * j, SUB), pl.ds(RO + 1 + SUB * j, SUB), pl.ds(RO - 1 + SUB * j, SUB)
         ro = pl.ds(SUB * j, SUB)
-        t = lt + 1
+        t, right, left = lt, lax.rem(lt + 1, 5), lax.rem(lt + 4, 5)
         c0 = cnt[lt, rc, :]
-        left = lax.rem(lt + 4, 5)
         luw = jnp.minimum(c0, west_of(c0, cnt[left, rc, :]))
         lvs = jnp.minimum(c0, cnt[lt, rs, :])
         lu = lu_o[lt, ro, :]
@@ -412,30 +506,30 @@
         yt, ys = zero8, zero8
         for k in range(NL):
             u = ub[t, k, rc, :]
-            me = jnp.where(lu > k, half_dt * u, ZERO)
-            mw = jnp.where(luw > k, half_dt * west_of(u, ub[t - 1, k, rc, :]), ZERO)
-            mn = jnp.where(lv > k, half_dt * vb[t, k, rc, :], ZERO)
-            ms = jnp.where(lvs > k, half_dt * vb[t, k, rs, :], ZERO)
+            me = keep(lu > k, half_dt * u)
+            mw = keep(luw > k, half_dt * uw_b[t, k, rc, :])
+            mn = keep(lv > k, half_dt * vb[t, k, rc, :])
+            ms = keep(lvs > k, half_dt * vb[t, k, rs, :])
 
             def advect(buf):
                 q = buf[t, k, rc, :]
-                qe = east_of(q, buf[t + 1, k, rc, :])
-                qw = west_of(q, buf[t - 1, k, rc, :])
+                qe = east_of(q, buf[right, k, rc, :])
+                qw = west_of(q, buf[left, k, rc, :])
                 qn = buf[t, k, rn, :]
                 qs = buf[t, k, rs, :]
                 return q - ((me * (q + qe) - mw * (qw + q)) + (mn * (q + qn) - ms * (qs + q)))
 
             qt = advect(tb)
             qs_ = advect(sb)
-            fac = jnp.where(c0 > k + 1, DIFF_IN[k], DIFF_END[k]) if k < NL - 1 else DIFF_END[k]
+            fac = pick(c0 > k + 1, DIFF_IN[k], DIFF_END[k]) if k < NL - 1 else DIFF_END[k]
             yt = jnp.where(c0 > k, (qt + yt) * fac, DIFF_R * qt)
             ys = jnp.where(c0 > k, (qs_ + ys) * fac, DIFF_R * qs_)
             tn_o[lt, k, ro, :] = yt
             sn_o[lt, k, ro, :] = ys
         xt, xs_ = zero8, zero8
         for k in reversed(range(NL)):
-            xt = tn_o[lt, k, ro, :] + (jnp.where(c0 > k + 1, DIFF_IN[k] * xt, ZERO) if k < NL - 1 else ZERO)
-            xs_ = sn_o[lt, k, ro, :] + (jnp.where(c0 > k + 1, DIFF_IN[k] * xs_, ZERO) if k < NL - 1 else ZERO)
+            xt = tn_o[lt, k, ro, :] + (keep(c0 > k + 1, DIFF_IN[k] * xt) if k < NL - 1 else ZERO)
+            xs_ = sn_o[lt, k, ro, :] + (keep(c0 > k + 1, DIFF_IN[k] * xs_) if k < NL - 1 else ZERO)
             tn_o[lt, k, ro, :] = (ONE / DIFF_R) * xt
             sn_o[lt, k, ro, :] = (ONE / DIFF_R) * xs_
 
@@ -444,12 +538,23 @@
         return 0
     lax.fori_loop(0, 16, tracers_all, 0)
 
+    z_wide[1].wait_recv()
     z_force.wait_recv()
-    arrived(n_far + n_force, s_far + s_force)
+    pl.when(far_s)(n_far.wait_recv)
+    pl.when(far_n)(s_far.wait_recv)
+    pl.when(down)(n_leg2.wait_recv)
+    pl.when(up)(s_leg2.wait_recv)
+    arrived([n_cor] + n_force, [s_cor] + s_force)
 
     for cp in z_wide + [z_col, z_force]:
         cp.wait_send()
-    both(s_first + s_vel + s_tra + s_far + s_force, n_first + n_vel + n_tra + n_far + n_force, lambda cp: cp.wait_send())
+    both(s_first + s_vel + s_tra + [s_cor] + s_force, n_first + n_vel + n_tra + [n_cor] + n_force, lambda cp: cp.wait_send())
+    pl.when(far_n)(n_far.wait_send)
+    pl.when(far_s)(s_far.wait_send)
+    pl.when(up)(n_leg1.wait_send)
+    pl.when(down)(s_leg1.wait_send)
+    pl.when(last_row)(n_leg2.wait_send)
+    pl.when(first_row)(s_leg2.wait_send)
 
 
 def finish_kernel(n_row, n_sub, w_ref,
@@ -460,6 +565,7 @@
     dtb = TIME_STEP / n_sub
     total_rows = float(n_row * NR)
     zero8 = jnp.zeros((SUB, LANE), F32)
+    west_of, east_of = movers()
     copies = []
 
     def put(src, dst):
@@ -606,15 +712,18 @@
             in_specs=[hbm] * 9,
             out_specs=[vmem] * len(outs),
             scratch_shapes=[
-                pltpu.VMEM((4, 6, NL, RO + NR + SUB, LANE), F32),
-                pltpu.VMEM((6, NL, RO + NR + SUB, LANE), F32),
-                pltpu.VMEM((5, RO + NR + SUB, LANE), F32),
-                pltpu.VMEM((3, NR, LANE), F32),
+                pltpu.VMEM((4, 5, NL, RO + NR + SUB, LANE), F32),
+                pltpu.VMEM((5, NL, RO + NR + SUB, LANE), F32),
+                pltpu.VMEM((NT, NL, RO + NR + SUB, LANE), F32),
+                pltpu.VMEM((NT, NL, RO + NR + SUB, LANE), F32),
+                pltpu.VMEM((2, 5, RO + NR + SUB, LANE), F32),
+                pltpu.VMEM((4, NT, NH, LANE), F32),
+                pltpu.VMEM((4, NR, LANE), F32),
                 pltpu.VMEM((NT, NR, LANE), jnp.int32),
                 pltpu.VMEM((4, 2, SUB, LANE), F32),
                 pltpu.VMEM((4, 2, SUB, LANE), F32),
                 pltpu.VMEM((NR, LANE), F32),
-                sems((16,)), sems((20,)), sems((N_COPY,)), sems((N_COPY,)),
+                sems((16,)), sems((24,)), sems((N_COPY,)), sems((N_COPY,)),
             ],
             compiler_params=pltpu.CompilerParams(collective_id=0, has_side_effects=True, vmem_limit_bytes=VMEM_MAIN),
             name='ocean',

time: 36.2 us -> 35 us (0.967)
  Pallas kernels: 35.5 us -> 34.2 us
    pallas_call x1, Pallas kernels: 24 us -> 22.7 us  [step(): pl.pallas_call(functools.partial(ocean_kernel, n_row, n_sub), out_shape=o...]
where the time goes in v3:
time: 35 us; the launch traced here: 34.9 us
  Pallas kernels  34.2 us (98%)
  between operations  0.66 us (2%)
    pallas_call x1, Pallas kernels, step(): pl.pallas_call(functools.partial(ocean_kernel, n_row, n_sub), out_shape=o...  22.7 us
    pallas_call x1, Pallas kernels, step(): pl.pallas_call(functools.partial(finish_kernel, n_row, n_sub), out_shape=...  11.5 us

profile of v3, /device:TPU:0, one launch (start us, length us, event | category | flops | bytes accessed | tf_op | source)
XLA Modules:
  0.0 34.9 jit_solution(8996558295040854265)
XLA Ops:
  0.6 0.0 copy-start
  0.6 22.7 %ocean.1 = (f32[4,31,32,128]{3,2,1,0:T(8,128)S(1)}, f32[4,31,32,128]{3,2,1,0:T(8,128)S(1)}, f32[4,31,32,128]{3,2,1,0:T(8,128)S(1)}, f32[4,31,32,128]{3,2,1,0:T(8...) custom-call(f32[31,32,512]{2,1,0:T(8,128)} %u_in.1, ...), custom_call_target="tpu_custom_call" | custom-call | tf_op jit(solution)/shard_map/ocean/pallas_call | solution.py:709
  23.4 0.0 copy-done
  23.4 11.5 %finish.1 = (f32[32,512]{1,0:T(8,128)}, f32[32,512]{1,0:T(8,128)}, f32[32,512]{1,0:T(8,128)}, f32[31,32,512]{2,1,0:T(8,128)}, f32[31,32,512]{2,1,0:T(8,128)}, /*...) custom-call(f32[30]{0:T(128)S(1)} %copy-done, f32[4,31,32,128]{3,2,1,0:T(8,128)S(1)} %get-tuple-element.19.us, ...), custom_call_target="tpu_custom_call" | custom-call | tf_op jit(solution)/shard_map/finish/pallas_call | solution.py:733
Async XLA Ops:
  0.6 22.7 %copy-start = (f32[30]{0:T(128)S(1)}, f32[30]{0:T(128)}, u32[]{:S(2)}) copy-start(f32[30]{0:T(128)} %w_ref.1) | copy-start | bytes 364

commit v4 on v3

--- a/solution.py
+++ b/solution.py
@@ -31,6 +31,8 @@
 WO = 40
 WR = 112
 N_COPY = 40
+LATE = 2
+T_TILES = 4
 NH = 30
 VMEM_MAIN = 40 * 1024 * 1024
 VMEM_FINISH = 12 * 1024 * 1024
@@ -68,8 +70,8 @@
     return west_of, east_of
 
 
-def corio(first, total_rows):
-    pos = (first + lax.broadcasted_iota(jnp.int32, (SUB, LANE), 0)).astype(F32)
+def corio(first, total_rows, height=SUB):
+    pos = (first + lax.broadcasted_iota(jnp.int32, (height, LANE), 0)).astype(F32)
     fu = CORIO_F0 + CORIO_BETA * ((pos + 0.5) / total_rows - 0.5)
     fv = CORIO_F0 + CORIO_BETA * ((pos + ONE) / total_rows - 0.5)
     return fu, fv
@@ -318,11 +320,8 @@
     s_tra = [rows3(2, low, north, -1), rows3(3, low, north, -1)]
     n_far, s_far = rows2(wide, 0, 4, n_src, n_dst, 1), rows2(wide, 0, 4, s_src, s_dst, -1)
     n_cor, s_cor = corner(n_src, n_dst, 1), corner(s_src, s_dst, -1)
-    both(s_tra, n_tra, lambda cp: cp.start())
+    both(s_tra, [], lambda cp: cp.start())
     far_n, far_s = jnp.logical_and(has_n, jnp.logical_not(up)), jnp.logical_and(has_s, jnp.logical_not(down))
-    pl.when(far_n)(n_far.start)
-    pl.when(far_s)(s_far.start)
-    both([s_cor], [n_cor], lambda cp: cp.start())
     lax.fori_loop(0, 2, pack, 0)
     z_col = remote(pk_s, pk_r, dev(0, ocol))
     z_col.start()
@@ -342,27 +341,35 @@
         return 0
     lax.fori_loop(0, NT, pressure_own, 0)
 
-    def near2d(buf, first, t):
-        c = buf[t, pl.ds(first, SUB), :]
-        return c, east_of(c, buf[t + 1, pl.ds(first, SUB), :]), buf[t, pl.ds(first + 1, SUB), :]
-
-    def pick(mask, inner, last):
-        return lax.select(mask, jnp.full((SUB, LANE), inner, F32), jnp.full((SUB, LANE), last, F32))
-
-    def keep(mask, value):
-        return lax.select(mask, value, zero8)
-
-    def momentum(lt, j, at_south=False, at_north=False):
-        rc, rn, rs = pl.ds(RO + SUB * j, SUB), pl.ds(RO + 1 + SUB * j, SUB), pl.ds(RO - 1 + SUB * j, SUB)
-        ro = pl.ds(SUB * j, SUB)
+    def chooser(height):
+        nothing = jnp.zeros((height, LANE), F32)
+
+        def pick(mask, inner, last):
+            return lax.select(mask, jnp.full((height, LANE), inner, F32), jnp.full((height, LANE), last, F32))
+
+        def keep(mask, value):
+            return lax.select(mask, value, nothing)
+
+        return nothing, pick, keep
+
+    def momentum(lt, j, height=SUB, at_south=False, at_north=False):
+        west_of, east_of = movers(height)
+        zero8, pick, keep = chooser(height)
+
+        def near2d(buf):
+            c = buf[lt, rc, :]
+            return c, east_of(c, buf[lt + 1, rc, :]), buf[lt, rn, :]
+
+        rc, rn, rs = pl.ds(RO + SUB * j, height), pl.ds(RO + 1 + SUB * j, height), pl.ds(RO - 1 + SUB * j, height)
+        ro = pl.ds(SUB * j, height)
         t, right, left = lt, lax.rem(lt + 1, 5), lax.rem(lt + 4, 5)
-        fu, fv = corio(row * NR + SUB * j, total_rows)
+        fu, fv = corio(row * NR + SUB * j, total_rows, height)
         fu4 = 0.25 * fu
         fv4 = 0.25 * fv
-        c0, ce, cn = near2d(cnt, RO + SUB * j, lt)
+        c0, ce, cn = near2d(cnt)
         lu = jnp.minimum(c0, ce)
         lv = jnp.minimum(c0, cn)
-        d0, de, dn = near2d(depth, RO + SUB * j, lt)
+        d0, de, dn = near2d(depth)
         hu = 0.5 * (d0 + de)
         hv = 0.5 * (d0 + dn)
         lu_o[lt, ro, :] = lu
@@ -393,15 +400,16 @@
             vstar = v - (u4 * (fv4 + 0.125 * (ve - vw)) + 0.5 * v * (vn - vs) + (pn - p))
             yu = (ustar + yu) * (pick(lu > k + 1, VISC_IN[k], VISC_END[k]) if k < NL - 1 else VISC_END[k])
             yv = (vstar + yv) * (pick(lv > k + 1, VISC_IN[k], VISC_END[k]) if k < NL - 1 else VISC_END[k])
-            us_o[lt, k, ro, :] = yu
-            vs_o[lt, k, ro, :] = yv
+            if k < NL - 1:
+                us_o[lt, k, ro, :] = yu
+                vs_o[lt, k, ro, :] = yv
             su = su + keep(lu > k, u)
             sv = sv + keep(lv > k, v)
         mu, mv = zero8, zero8
         xu, xv = zero8, zero8
         for k in reversed(range(NL)):
-            xu = us_o[lt, k, ro, :] + (keep(lu > k + 1, VISC_IN[k] * xu) if k < NL - 1 else ZERO)
-            xv = vs_o[lt, k, ro, :] + (keep(lv > k + 1, VISC_IN[k] * xv) if k < NL - 1 else ZERO)
+            xu = yu if k == NL - 1 else us_o[lt, k, ro, :] + (keep(lu > k + 1, VISC_IN[k] * xu))
+            xv = yv if k == NL - 1 else vs_o[lt, k, ro, :] + (keep(lv > k + 1, VISC_IN[k] * xv))
             outu = (ONE / VISC_R) * xu
             outv = (ONE / VISC_R) * xv
             us_o[lt, k, ro, :] = outu
@@ -413,24 +421,31 @@
         mu_s[lt, ro, :] = mu * iu
         mv_s[lt, ro, :] = mv * iv
         scale = dtb * dtb / TIME_STEP
-        rw = pl.ds(WO + SUB * j, SUB)
+        rw = pl.ds(WO + SUB * j, height)
         abuf[0, lt, rw, :] = jnp.where(lu > ZERO, scale * hu * ((mu - su) * iu), ZERO)
         abuf[1, lt, rw, :] = jnp.where(lv > ZERO, scale * hv * ((mv - sv) * iv), ZERO)
 
     def middle_rows(i, _):
-        odd, later = lax.rem(i, 2), i // 4
-
-        @pl.when(jnp.logical_and(i == 6, last_row))
+        odd, later = lax.rem(i, 2), i // 2
+
+        @pl.when(jnp.logical_and(i == 3, last_row))
         def _():
             n_leg1.wait_recv()
             n_leg2.start()
 
-        @pl.when(jnp.logical_and(i == 6, first_row))
+        @pl.when(jnp.logical_and(i == 3, first_row))
         def _():
             s_leg1.wait_recv()
             s_leg2.start()
 
-        @pl.when(i == 4)
+        @pl.when(i == LATE)
+        def _():
+            both([], n_tra, lambda cp: cp.start())
+            pl.when(far_n)(n_far.start)
+            pl.when(far_s)(s_far.start)
+            both([s_cor], [n_cor], lambda cp: cp.start())
+
+        @pl.when(i == 2)
         def _():
             for cp in (z_wide[0], z_col):
                 cp.wait_recv()
@@ -439,10 +454,10 @@
             shift_v(3)
             pressure(4, all_rows, NR)
 
-        momentum(1 + odd + later * (2 * odd - 1), 1 + lax.rem(i, 4) // 2)
-        return 0
-
-    lax.fori_loop(0, SUB, middle_rows, 0)
+        momentum(1 + odd + later * (2 * odd - 1), 1, 2 * SUB)
+        return 0
+
+    lax.fori_loop(0, NT, middle_rows, 0)
 
     arrived(n_first + n_vel, s_first + s_vel + s_tra)
 
@@ -493,9 +508,11 @@
 
     arrived(n_tra, [])
 
-    def tracers(lt, j):
-        rc, rn, rs = pl.ds(RO + SUB * j, SUB), pl.ds(RO + 1 + SUB * j, SUB), pl.ds(RO - 1 + SUB * j, SUB)
-        ro = pl.ds(SUB * j, SUB)
+    def tracers(lt, j, height):
+        west_of, east_of = movers(height)
+        zero8, pick, keep = chooser(height)
+        rc, rn, rs = pl.ds(RO + SUB * j, height), pl.ds(RO + 1 + SUB * j, height), pl.ds(RO - 1 + SUB * j, height)
+        ro = pl.ds(SUB * j, height)
         t, right, left = lt, lax.rem(lt + 1, 5), lax.rem(lt + 4, 5)
         c0 = cnt[lt, rc, :]
         luw = jnp.minimum(c0, west_of(c0, cnt[left, rc, :]))
@@ -506,10 +523,10 @@
         yt, ys = zero8, zero8
         for k in range(NL):
             u = ub[t, k, rc, :]
-            me = keep(lu > k, half_dt * u)
-            mw = keep(luw > k, half_dt * uw_b[t, k, rc, :])
-            mn = keep(lv > k, half_dt * vb[t, k, rc, :])
-            ms = keep(lvs > k, half_dt * vb[t, k, rs, :])
+            me = keep(lu > k, u)
+            mw = keep(luw > k, uw_b[t, k, rc, :])
+            mn = keep(lv > k, vb[t, k, rc, :])
+            ms = keep(lvs > k, vb[t, k, rs, :])
 
             def advect(buf):
                 q = buf[t, k, rc, :]
@@ -517,26 +534,27 @@
                 qw = west_of(q, buf[left, k, rc, :])
                 qn = buf[t, k, rn, :]
                 qs = buf[t, k, rs, :]
-                return q - ((me * (q + qe) - mw * (qw + q)) + (mn * (q + qn) - ms * (qs + q)))
+                return q - half_dt * ((me * (q + qe) - mw * (qw + q)) + (mn * (q + qn) - ms * (qs + q)))
 
             qt = advect(tb)
             qs_ = advect(sb)
             fac = pick(c0 > k + 1, DIFF_IN[k], DIFF_END[k]) if k < NL - 1 else DIFF_END[k]
             yt = jnp.where(c0 > k, (qt + yt) * fac, DIFF_R * qt)
             ys = jnp.where(c0 > k, (qs_ + ys) * fac, DIFF_R * qs_)
-            tn_o[lt, k, ro, :] = yt
-            sn_o[lt, k, ro, :] = ys
+            if k < NL - 1:
+                tn_o[lt, k, ro, :] = yt
+                sn_o[lt, k, ro, :] = ys
         xt, xs_ = zero8, zero8
         for k in reversed(range(NL)):
-            xt = tn_o[lt, k, ro, :] + (keep(c0 > k + 1, DIFF_IN[k] * xt) if k < NL - 1 else ZERO)
-            xs_ = sn_o[lt, k, ro, :] + (keep(c0 > k + 1, DIFF_IN[k] * xs_) if k < NL - 1 else ZERO)
+            xt = yt if k == NL - 1 else tn_o[lt, k, ro, :] + (keep(c0 > k + 1, DIFF_IN[k] * xt))
+            xs_ = ys if k == NL - 1 else sn_o[lt, k, ro, :] + (keep(c0 > k + 1, DIFF_IN[k] * xs_))
             tn_o[lt, k, ro, :] = (ONE / DIFF_R) * xt
             sn_o[lt, k, ro, :] = (ONE / DIFF_R) * xs_
 
     def tracers_all(i, _):
-        tracers(lax.rem(i, 4), i // 4)
-        return 0
-    lax.fori_loop(0, 16, tracers_all, 0)
+        tracers(lax.rem(i, NT), T_TILES * (i // NT), T_TILES * SUB)
+        return 0
+    lax.fori_loop(0, 16 // T_TILES, tracers_all, 0)
 
     z_wide[1].wait_recv()
     z_force.wait_recv()
@@ -587,16 +605,16 @@
         inside = place >= 0
         wet_u = jnp.logical_and(inside, place < n_row * NR).astype(F32)
         wet_v = jnp.logical_and(inside, place < n_row * NR - 1).astype(F32)
+        cfu[rows, :] = wet_u * ((0.25 * dtb) * fu)
+        cfv[rows, :] = wet_v * ((0.25 * dtb) * fv)
+        mku[rows, :] = wet_u
+        mkv[rows, :] = wet_v
         for t in range(5):
             right = (t + 1) % 5
             d0 = wide[3, t, rows, :]
             scale = 0.5 * dtb * dtb * GRAVITY
             bu[t, rows, :] = wet_u * (scale * (d0 + east_of(d0, wide[3, right, rows, :])))
             bv[t, rows, :] = wet_v * (scale * (d0 + wide[3, t, rown, :]))
-            cfu[t, rows, :] = wet_u * ((0.25 * dtb) * fu)
-            cfv[t, rows, :] = wet_v * ((0.25 * dtb) * fv)
-            mku[t, rows, :] = wet_u
-            mkv[t, rows, :] = wet_v
             tu[0, t, rows, :] = dtb * wide[2, t, rows, :]
             tv[0, t, rows, :] = dtb * wide[1, t, rows, :]
         return 0
@@ -614,40 +632,46 @@
     def subcycle(n, cur, lo, hi, first=False):
         nxt = 1 - cur
         weight = w_ref[n] * (ONE / dtb)
-        for i in range(lo, hi):
-            rows = pl.ds(SUB + SUB * i, SUB)
+        def eta_part(i):
+            rows, rows_s = pl.ds(SUB + SUB * i, SUB), pl.ds(7 + SUB * i, SUB)
+            u0 = [tu[cur, t, rows, :] for t in range(5)]
+            v0 = [tv[cur, t, rows, :] for t in range(5)]
+            vs = [tv[cur, t, rows_s, :] for t in range(5)]
+            uw = [west_of(u0[t], u0[(t + 4) % 5]) for t in range(5)]
+            u2 = [u0[t] + uw[t] for t in range(5)]
+            es = [wide[0, t, rows, :] - ((u0[t] - uw[t]) + (v0[t] - vs[t])) for t in range(5)]
+            for t in range(5):
+                wide[0, t, rows, :] = es[t]
+                xs[t, rows, :] = u2[t]
+
+        def flow_part(i):
+            rows, rows_n = pl.ds(SUB + SUB * i, SUB), pl.ds(9 + SUB * i, SUB)
+            f_u, f_v = cfu[rows, :], cfv[rows, :]
             rows_s = pl.ds(7 + SUB * i, SUB)
-            us = [tu[cur, t, rows, :] for t in range(5)]
-            for t in range(5):
-                uw = west_of(us[t], us[(t + 4) % 5])
-                xs[t, rows, :] = us[t] + uw
-                wide[0, t, rows, :] = wide[0, t, rows, :] - ((us[t] - uw) + (tv[cur, t, rows, :] - tv[cur, t, rows_s, :]))
-        for i in range(lo, hi):
-            rows = pl.ds(SUB + SUB * i, SUB)
-            rows_s = pl.ds(7 + SUB * i, SUB)
-            rows_n = pl.ds(9 + SUB * i, SUB)
-            es = [wide[0, t, rows, :] for t in range(5)]
             v0 = [tv[cur, t, rows, :] for t in range(5)]
             v2 = [v0[t] + tv[cur, t, rows_s, :] for t in range(5)]
+            v4 = [v2[t] + east_of(v2[t], v2[(t + 1) % 5]) for t in range(5)]
+            es = [wide[0, t, rows, :] for t in range(5)]
             for t in range(5):
-                right = (t + 1) % 5
-                v4 = v2[t] + east_of(v2[t], v2[right])
-                slope_u = east_of(es[t], es[right]) - es[t]
+                slope_u = east_of(es[t], es[(t + 1) % 5]) - es[t]
                 slope_v = wide[0, t, rows_n, :] - es[t]
                 u4 = xs[t, rows, :] + xs[t, rows_n, :]
-                u_old = tu[cur, t, rows, :]
-                v_old = v0[t]
+                u_old, v_old = tu[cur, t, rows, :], tv[cur, t, rows, :]
                 if first:
-                    u_old = mku[t, rows, :] * u_old
-                    v_old = mkv[t, rows, :] * v_old
-                u_new = (u_old + abuf[0, t, rows, :]) + (cfu[t, rows, :] * v4 - bu[t, rows, :] * slope_u)
-                v_new = (v_old + abuf[1, t, rows, :]) - (cfv[t, rows, :] * u4 + bv[t, rows, :] * slope_v)
+                    u_old = mku[rows, :] * u_old
+                    v_old = mkv[rows, :] * v_old
+                u_new = (u_old + abuf[0, t, rows, :]) + (f_u * v4[t] - bu[t, rows, :] * slope_u)
+                v_new = (v_old + abuf[1, t, rows, :]) - (f_v * u4 + bv[t, rows, :] * slope_v)
                 tu[nxt, t, rows, :] = u_new
                 tv[nxt, t, rows, :] = v_new
                 if 4 <= i < SUB and t < NT:
                     ro = pl.ds(SUB * (i - 4), SUB)
                     acu[t, ro, :] += weight * u_new
                     acv[t, ro, :] += weight * v_new
+
+        for part in (eta_part, flow_part):
+            for i in reversed(range(lo, hi)):
+                part(i)
 
     def pairs(first_n, count, lo, hi):
         def body(i, _):
@@ -735,7 +759,7 @@
             out_shape=[flat] * 3 + [cube] * 4,
             in_specs=[smem] + [vmem] * len(outs),
             out_specs=[hbm] * 7,
-            scratch_shapes=[wide1] * 6 + [force_v, force_v, wide1] + [flat_v] * 4 + [pltpu.VMEM((3, NT, NR, LANE), F32), cube_v, cube_v, sems((28,))],
+            scratch_shapes=[wide1] * 2 + [pltpu.VMEM((WR, LANE), F32)] * 4 + [force_v, force_v, wide1] + [flat_v] * 4 + [pltpu.VMEM((3, NT, NR, LANE), F32), cube_v, cube_v, sems((28,))],
             compiler_params=pltpu.CompilerParams(vmem_limit_bytes=VMEM_FINISH),
             name='finish',
         )(avg_weights, *mids)

time: 35 us -> 33.3 us (0.951)
  Pallas kernels: 34.2 us -> 32.5 us
    pallas_call x1, Pallas kernels: 22.7 us -> 21.3 us  [step(): pl.pallas_call(functools.partial(ocean_kernel, n_row, n_sub), out_shape=o...]
where the time goes in v4:
time: 33.3 us; the launch traced here: 33.2 us
  Pallas kernels  32.5 us (98%)
  between operations  0.66 us (2%)
    pallas_call x1, Pallas kernels, step(): pl.pallas_call(functools.partial(ocean_kernel, n_row, n_sub), out_shape=o...  21.3 us
    pallas_call x1, Pallas kernels, step(): pl.pallas_call(functools.partial(finish_kernel, n_row, n_sub), out_shape=...  11.2 us

profile of v4, /device:TPU:0, one launch (start us, length us, event | category | flops | bytes accessed | tf_op | source)
XLA Modules:
  0.0 33.2 jit_solution(9463391066809591108)
XLA Ops:
  0.6 0.0 copy-start
  0.6 21.3 %ocean.1 = (f32[4,31,32,128]{3,2,1,0:T(8,128)S(1)}, f32[4,31,32,128]{3,2,1,0:T(8,128)S(1)}, f32[4,31,32,128]{3,2,1,0:T(8,128)S(1)}, f32[4,31,32,128]{3,2,1,0:T(8...) custom-call(f32[31,32,512]{2,1,0:T(8,128)} %u_in.1, ...), custom_call_target="tpu_custom_call" | custom-call | tf_op jit(solution)/shard_map/ocean/pallas_call | solution.py:733
  22.0 0.0 copy-done
  22.0 11.2 %finish.1 = (f32[32,512]{1,0:T(8,128)}, f32[32,512]{1,0:T(8,128)}, f32[32,512]{1,0:T(8,128)}, f32[31,32,512]{2,1,0:T(8,128)}, f32[31,32,512]{2,1,0:T(8,128)}, /*...) custom-call(f32[30]{0:T(128)S(1)} %copy-done, f32[4,31,32,128]{3,2,1,0:T(8,128)S(1)} %get-tuple-element.19.us, ...), custom_call_target="tpu_custom_call" | custom-call | tf_op jit(solution)/shard_map/finish/pallas_call | solution.py:757
Async XLA Ops:
  0.6 21.3 %copy-start = (f32[30]{0:T(128)S(1)}, f32[30]{0:T(128)}, u32[]{:S(2)}) copy-start(f32[30]{0:T(128)} %w_ref.1) | copy-start | bytes 364

commit v5 on v4

--- a/solution.py
+++ b/solution.py
@@ -410,12 +410,11 @@
         for k in reversed(range(NL)):
             xu = yu if k == NL - 1 else us_o[lt, k, ro, :] + (keep(lu > k + 1, VISC_IN[k] * xu))
             xv = yv if k == NL - 1 else vs_o[lt, k, ro, :] + (keep(lv > k + 1, VISC_IN[k] * xv))
-            outu = (ONE / VISC_R) * xu
-            outv = (ONE / VISC_R) * xv
-            us_o[lt, k, ro, :] = outu
-            vs_o[lt, k, ro, :] = outv
-            mu = mu + keep(lu > k, outu)
-            mv = mv + keep(lv > k, outv)
+            us_o[lt, k, ro, :] = xu
+            vs_o[lt, k, ro, :] = xv
+            mu = mu + keep(lu > k, xu)
+            mv = mv + keep(lv > k, xv)
+        mu, mv = (ONE / VISC_R) * mu, (ONE / VISC_R) * mv
         iu = ONE / jnp.maximum(lu, ONE)
         iv = ONE / jnp.maximum(lv, ONE)
         mu_s[lt, ro, :] = mu * iu
@@ -519,37 +518,34 @@
         lvs = jnp.minimum(c0, cnt[lt, rs, :])
         lu = lu_o[lt, ro, :]
         lv = lv_o[lt, ro, :]
-        half_dt = 0.5 * TIME_STEP
         yt, ys = zero8, zero8
         for k in range(NL):
-            u = ub[t, k, rc, :]
-            me = keep(lu > k, u)
+            here = c0 > k
+            me = keep(lu > k, ub[t, k, rc, :])
             mw = keep(luw > k, uw_b[t, k, rc, :])
             mn = keep(lv > k, vb[t, k, rc, :])
             ms = keep(lvs > k, vb[t, k, rs, :])
+            own = 2.0 - ((me - mw) + (mn - ms))
 
             def advect(buf):
                 q = buf[t, k, rc, :]
                 qe = east_of(q, buf[right, k, rc, :])
                 qw = west_of(q, buf[left, k, rc, :])
-                qn = buf[t, k, rn, :]
-                qs = buf[t, k, rs, :]
-                return q - half_dt * ((me * (q + qe) - mw * (qw + q)) + (mn * (q + qn) - ms * (qs + q)))
-
-            qt = advect(tb)
-            qs_ = advect(sb)
-            fac = pick(c0 > k + 1, DIFF_IN[k], DIFF_END[k]) if k < NL - 1 else DIFF_END[k]
-            yt = jnp.where(c0 > k, (qt + yt) * fac, DIFF_R * qt)
-            ys = jnp.where(c0 > k, (qs_ + ys) * fac, DIFF_R * qs_)
+                return (own * q + (mw * qw - me * qe)) + (ms * buf[t, k, rs, :] - mn * buf[t, k, rn, :])
+
+            end = pick(here, DIFF_END[k], 0.5)
+            fac = lax.select(c0 > k + 1, jnp.full_like(end, DIFF_IN[k]), end) if k < NL - 1 else end
+            yt = (advect(tb) + keep(here, yt)) * fac
+            ys = (advect(sb) + keep(here, ys)) * fac
             if k < NL - 1:
                 tn_o[lt, k, ro, :] = yt
                 sn_o[lt, k, ro, :] = ys
         xt, xs_ = zero8, zero8
         for k in reversed(range(NL)):
-            xt = yt if k == NL - 1 else tn_o[lt, k, ro, :] + (keep(c0 > k + 1, DIFF_IN[k] * xt))
-            xs_ = ys if k == NL - 1 else sn_o[lt, k, ro, :] + (keep(c0 > k + 1, DIFF_IN[k] * xs_))
-            tn_o[lt, k, ro, :] = (ONE / DIFF_R) * xt
-            sn_o[lt, k, ro, :] = (ONE / DIFF_R) * xs_
+            xt = yt if k == NL - 1 else tn_o[lt, k, ro, :] + keep(c0 > k + 1, DIFF_IN[k] * xt)
+            xs_ = ys if k == NL - 1 else sn_o[lt, k, ro, :] + keep(c0 > k + 1, DIFF_IN[k] * xs_)
+            tn_o[lt, k, ro, :] = xt
+            sn_o[lt, k, ro, :] = xs_
 
     def tracers_all(i, _):
         tracers(lax.rem(i, NT), T_TILES * (i // NT), T_TILES * SUB)
@@ -595,7 +591,7 @@
         for t in range(NT):
             put(src.at[t], dst.at[:, :, pl.ds(LANE * t, LANE)])
 
-    def setup(i, _):
+    def setup(i):
         base = SUB + SUB * i
         rows = pl.ds(base, SUB)
         rown = pl.ds(base + 1, SUB)
@@ -617,14 +613,14 @@
             bv[t, rows, :] = wet_v * (scale * (d0 + wide[3, t, rown, :]))
             tu[0, t, rows, :] = dtb * wide[2, t, rows, :]
             tv[0, t, rows, :] = dtb * wide[1, t, rows, :]
-        return 0
 
     for i in range(12):
         rows = pl.ds(SUB + SUB * i, SUB)
         for f in range(2):
             wide[f + 2, 4, rows, :] = pltpu.roll(wide[f, 4, rows, :], LANE // 2, 1)
         abuf[1, 4, rows, :] = pltpu.roll(abuf[0, 4, rows, :], LANE // 2, 1)
-    lax.fori_loop(0, 12, setup, 0)
+    for i in range(12):
+        setup(i)
     for t in range(NT):
         acu[t] = jnp.zeros((NR, LANE), F32)
         acv[t] = jnp.zeros((NR, LANE), F32)
@@ -709,7 +705,7 @@
                 count = lev[t, ro, :]
                 shift = cor[t, ro, :]
                 for k in range(NL):
-                    buf[t, k, ro, :] = jnp.where(count > k, src[t, k, ro, :] + shift, ZERO)
+                    buf[t, k, ro, :] = jnp.where(count > k, (ONE / VISC_R) * src[t, k, ro, :] + shift, ZERO)
             put(buf.at[t], dst.at[:, :, pl.ds(LANE * t, LANE)])
     for cp in copies:
         cp.wait()

time: 33.3 us -> 32.1 us (0.964)
  Pallas kernels: 32.5 us -> 31.3 us
    pallas_call x1, Pallas kernels: 11.2 us -> 10.3 us  [step(): pl.pallas_call(functools.partial(finish_kernel, n_row, n_sub), out_shape=...]
where the time goes in v5:
time: 32.1 us; the launch traced here: 32 us
  Pallas kernels  31.3 us (98%)
  between operations  0.66 us (2%)
    pallas_call x1, Pallas kernels, step(): pl.pallas_call(functools.partial(ocean_kernel, n_row, n_sub), out_shape=o...  21 us
    pallas_call x1, Pallas kernels, step(): pl.pallas_call(functools.partial(finish_kernel, n_row, n_sub), out_shape=...  10.3 us

profile of v5, /device:TPU:0, one launch (start us, length us, event | category | flops | bytes accessed | tf_op | source)
XLA Modules:
  0.0 32.0 jit_solution(2105437588183779727)
XLA Ops:
  0.6 0.0 copy-start
  0.6 21.0 %ocean.1 = (f32[4,31,32,128]{3,2,1,0:T(8,128)S(1)}, f32[4,31,32,128]{3,2,1,0:T(8,128)S(1)}, f32[4,31,32,128]{3,2,1,0:T(8,128)S(1)}, f32[4,31,32,128]{3,2,1,0:T(8...) custom-call(f32[31,32,512]{2,1,0:T(8,128)} %u_in.1, ...), custom_call_target="tpu_custom_call" | custom-call | tf_op jit(solution)/shard_map/ocean/pallas_call | solution.py:729
  21.7 0.0 copy-done
  21.7 10.3 %finish.1 = (f32[32,512]{1,0:T(8,128)}, f32[32,512]{1,0:T(8,128)}, f32[32,512]{1,0:T(8,128)}, f32[31,32,512]{2,1,0:T(8,128)}, f32[31,32,512]{2,1,0:T(8,128)}, /*...) custom-call(f32[30]{0:T(128)S(1)} %copy-done, f32[4,31,32,128]{3,2,1,0:T(8,128)S(1)} %get-tuple-element.19.us, ...), custom_call_target="tpu_custom_call" | custom-call | tf_op jit(solution)/shard_map/finish/pallas_call | solution.py:753
Async XLA Ops:
  0.6 21.0 %copy-start = (f32[30]{0:T(128)S(1)}, f32[30]{0:T(128)}, u32[]{:S(2)}) copy-start(f32[30]{0:T(128)} %w_ref.1) | copy-start | bytes 364

commit v6 on v5

--- a/solution.py
+++ b/solution.py
@@ -259,6 +259,12 @@
         return (4 * k + j) // 64, 2 * ((4 * k + j) % 64)
 
     def pack(half_of, _):
+        @pl.when(half_of == 1)
+        def _():
+            for t in (0, 3):
+                for f in (2, 3):
+                    loads[f, t].wait()
+
         here = lanes()
         first = lax.broadcasted_iota(jnp.int32, (NR, LANE), 1) == 0
         acc = {}
@@ -313,18 +319,18 @@
         return 0
     lax.fori_loop(0, 3, shift_own, 0)
 
-    for t in (0, 3, 1, 2):
-        for f in (2, 3):
-            loads[f, t].wait()
     n_tra = [rows3(2, top, south, 1), rows3(3, top, south, 1)]
     s_tra = [rows3(2, low, north, -1), rows3(3, low, north, -1)]
     n_far, s_far = rows2(wide, 0, 4, n_src, n_dst, 1), rows2(wide, 0, 4, s_src, s_dst, -1)
     n_cor, s_cor = corner(n_src, n_dst, 1), corner(s_src, s_dst, -1)
-    both(s_tra, [], lambda cp: cp.start())
     far_n, far_s = jnp.logical_and(has_n, jnp.logical_not(up)), jnp.logical_and(has_s, jnp.logical_not(down))
     lax.fori_loop(0, 2, pack, 0)
     z_col = remote(pk_s, pk_r, dev(0, ocol))
     z_col.start()
+    for t in (1, 2):
+        for f in (2, 3):
+            loads[f, t].wait()
+    both(s_tra, [], lambda cp: cp.start())
 
     p_unit = 0.5 * BC_GRAVITY / NL
 

time: 32.1 us -> 31.9 us (level)
  no operation moved by 1% of the time
where the time goes in v6:
time: 31.9 us; the launch traced here: 31.7 us
  Pallas kernels  31.1 us (97%)
  between operations  0.66 us (2%)
    pallas_call x1, Pallas kernels, step(): pl.pallas_call(functools.partial(ocean_kernel, n_row, n_sub), out_shape=o...  20.8 us
    pallas_call x1, Pallas kernels, step(): pl.pallas_call(functools.partial(finish_kernel, n_row, n_sub), out_shape=...  10.3 us

profile of v6, /device:TPU:0, one launch (start us, length us, event | category | flops | bytes accessed | tf_op | source)
XLA Modules:
  0.0 31.7 jit_solution(12616811436712205939)
XLA Ops:
  0.6 0.0 copy-start
  0.6 20.8 %ocean.1 = (f32[4,31,32,128]{3,2,1,0:T(8,128)S(1)}, f32[4,31,32,128]{3,2,1,0:T(8,128)S(1)}, f32[4,31,32,128]{3,2,1,0:T(8,128)S(1)}, f32[4,31,32,128]{3,2,1,0:T(8...) custom-call(f32[31,32,512]{2,1,0:T(8,128)} %u_in.1, ...), custom_call_target="tpu_custom_call" | custom-call | tf_op jit(solution)/shard_map/ocean/pallas_call | solution.py:735
  21.4 0.0 copy-done
  21.4 10.3 %finish.1 = (f32[32,512]{1,0:T(8,128)}, f32[32,512]{1,0:T(8,128)}, f32[32,512]{1,0:T(8,128)}, f32[31,32,512]{2,1,0:T(8,128)}, f32[31,32,512]{2,1,0:T(8,128)}, /*...) custom-call(f32[30]{0:T(128)S(1)} %copy-done, f32[4,31,32,128]{3,2,1,0:T(8,128)S(1)} %get-tuple-element.19.us, ...), custom_call_target="tpu_custom_call" | custom-call | tf_op jit(solution)/shard_map/finish/pallas_call | solution.py:759
Async XLA Ops:
  0.6 20.8 %copy-start = (f32[30]{0:T(128)S(1)}, f32[30]{0:T(128)}, u32[]{:S(2)}) copy-start(f32[30]{0:T(128)} %w_ref.1) | copy-start | bytes 364

commit v7 on v6

--- a/solution.py
+++ b/solution.py
@@ -261,9 +261,10 @@
     def pack(half_of, _):
         @pl.when(half_of == 1)
         def _():
-            for t in (0, 3):
+            for t in (0, 3, 1, 2):
                 for f in (2, 3):
                     loads[f, t].wait()
+            both(s_tra, [], lambda cp: cp.start())
 
         here = lanes()
         first = lax.broadcasted_iota(jnp.int32, (NR, LANE), 1) == 0
@@ -327,10 +328,6 @@
     lax.fori_loop(0, 2, pack, 0)
     z_col = remote(pk_s, pk_r, dev(0, ocol))
     z_col.start()
-    for t in (1, 2):
-        for f in (2, 3):
-            loads[f, t].wait()
-    both(s_tra, [], lambda cp: cp.start())
 
     p_unit = 0.5 * BC_GRAVITY / NL
 

time: 31.9 us -> 31.9 us (level)
  no operation moved by 1% of the time
where the time goes in v7:
time: 31.9 us; the launch traced here: 31.7 us
  Pallas kernels  31.1 us (97%)
  between operations  0.66 us (2%)
    pallas_call x1, Pallas kernels, step(): pl.pallas_call(functools.partial(ocean_kernel, n_row, n_sub), out_shape=o...  20.8 us
    pallas_call x1, Pallas kernels, step(): pl.pallas_call(functools.partial(finish_kernel, n_row, n_sub), out_shape=...  10.3 us

profile of v7, /device:TPU:0, one launch (start us, length us, event | category | flops | bytes accessed | tf_op | source)
XLA Modules:
  0.0 31.7 jit_solution(9896554019027809370)
XLA Ops:
  0.6 0.0 copy-start
  0.6 20.8 %ocean.1 = (f32[4,31,32,128]{3,2,1,0:T(8,128)S(1)}, f32[4,31,32,128]{3,2,1,0:T(8,128)S(1)}, f32[4,31,32,128]{3,2,1,0:T(8,128)S(1)}, f32[4,31,32,128]{3,2,1,0:T(8...) custom-call(f32[31,32,512]{2,1,0:T(8,128)} %u_in.1, ...), custom_call_target="tpu_custom_call" | custom-call | tf_op jit(solution)/shard_map/ocean/pallas_call | solution.py:732
  21.4 0.0 copy-done
  21.4 10.3 %finish.1 = (f32[32,512]{1,0:T(8,128)}, f32[32,512]{1,0:T(8,128)}, f32[32,512]{1,0:T(8,128)}, f32[31,32,512]{2,1,0:T(8,128)}, f32[31,32,512]{2,1,0:T(8,128)}, /*...) custom-call(f32[30]{0:T(128)S(1)} %copy-done, f32[4,31,32,128]{3,2,1,0:T(8,128)S(1)} %get-tuple-element.19.us, ...), custom_call_target="tpu_custom_call" | custom-call | tf_op jit(solution)/shard_map/finish/pallas_call | solution.py:756
Async XLA Ops:
  0.6 20.8 %copy-start = (f32[30]{0:T(128)S(1)}, f32[30]{0:T(128)}, u32[]{:S(2)}) copy-start(f32[30]{0:T(128)} %w_ref.1) | copy-start | bytes 364
